TPU v7x, 32 devices: a whole 2x2x4 slice. The times are simulated.
32 devices in a mesh: dp: 8 (over z, y), rep: 4 (over x, core).
Axes of the slice: x: 2, y: 2, z: 4, core: 2. Of those that a mesh axis runs over, the one named last changes fastest.
Arguments:
- tokens: bfloat16 [32768, 768], P(('dp', 'rep')), may hold values from -6 to 6
- qkv_weight: bfloat16 [768, 2304], P('dp'), may hold values from -0.21875 to 0.21875
- out_weight: bfloat16 [768, 768], P('dp'), may hold values from -0.875 to 0.875
- up_weight: bfloat16 [768, 3072], P('dp'), may hold values from -0.21875 to 0.21875
- down_weight: bfloat16 [3072, 768], P('dp'), may hold values from -0.109375 to 0.109375
- norm_gains: bfloat16 [2, 768], P(None, 'dp'), may hold values from 0.5 to 1.5
- bias_rows: bfloat16 [6, 768], P(None, 'dp'), may hold values from -3 to 3
- ff_bias: bfloat16 [3072], P('dp'), may hold values from -3 to 3
- lengths: int32 [288], replicated, may hold values from 32 to 512, as said below
- owners: int32 [288], replicated, may hold values from 0 to 31, as said below
- cotangent: bfloat16 [32768, 768], P(('dp', 'rep')), may hold values from -6 to 6
Outputs:
- output: bfloat16 [32768, 768], P(('dp', 'rep'))
- grad_tokens: float32 [32768, 768], P(('dp', 'rep'))
- grad_qkv: float32 [768, 2304], P('dp')
- grad_out_weight: float32 [768, 768], P('dp')
- grad_up_weight: float32 [768, 3072], P('dp')
- grad_down_weight: float32 [3072, 768], P('dp')
- grad_norm_gains: float32 [2, 768], P(None, 'dp')
- grad_bias_rows: float32 [6, 768], P(None, 'dp')
- grad_ff_bias: float32 [3072], P('dp')
Inputs may be any that keep to these rules, and one draw needn't show every extreme that they name: Passage p holds lengths[p] tokens and belongs to device owners[p]. Every device holds exactly 9 passages, at most one of them longer than 64; a device's passages hold at most 1024 tokens together, and some device's hold exactly 1024. `owners`: each device number appears exactly 9 times.
All inputs are finite; a program needn't handle non-finite values.
Results may differ from a plain program's by a relative error of at most 0.017.
Values may be sent and summed in bfloat16 or wider, within the bound.
A program may use at most 192 MiB of HBM per device.

v0:
```python
import jax
import jax.numpy as jnp
from jax import lax
from jax.sharding import PartitionSpec as P

HEADS = 12
HD = 64


norm_eps = 1e-06
masked_score = -1000000000.0


def token_segments(lengths, owners, device, row_count):
    own_mask = owners == device
    own_sizes = jnp.where(own_mask, lengths, 0)
    end_points = jnp.cumsum(own_sizes)
    start_points = jnp.where(own_mask, end_points - own_sizes, row_count)
    start_marks = (
        jnp.zeros((row_count + 1,), jnp.int32).at[start_points].add(jnp.ones_like(start_points))
    )
    segment = jnp.cumsum(start_marks[:row_count])
    live_rows = jnp.arange(row_count, dtype=jnp.int32) < end_points[-1]
    return (segment, live_rows)


def normalize_keep(residual, gain_row, shift_row):
    center = residual - jnp.mean(residual, axis=-1, keepdims=True)
    scale_inv = lax.rsqrt(jnp.mean(center * center, axis=-1, keepdims=True) + norm_eps)
    unit_rows = center * scale_inv
    return (unit_rows * gain_row + shift_row, unit_rows, scale_inv)


def normalize_back(grad_in, unit_rows, scale_inv, gain_row):
    scaled = grad_in * gain_row
    return scale_inv * (
        scaled
        - jnp.mean(scaled, axis=-1, keepdims=True)
        - unit_rows * jnp.mean(scaled * unit_rows, axis=-1, keepdims=True)
    )


def allowed_block(segment, live_rows, row_start, query_block):
    row_count = segment.shape[0]
    stop_row = row_start + query_block
    same_segment = (
        (segment[row_start:stop_row, None] == segment[None, :])
        & live_rows[row_start:stop_row, None]
        & live_rows[None, :]
    )
    self_pair = jnp.arange(query_block)[:, None] + row_start == jnp.arange(row_count)[None, :]
    return (same_segment | self_pair)[None]


def split_pairs(matrix, head_pairs):
    row_count = matrix.shape[0]
    return matrix.reshape(row_count, head_pairs, -1).transpose(1, 0, 2)


def join_pairs(stacked):
    row_count = stacked.shape[1]
    return stacked.transpose(1, 0, 2).reshape(row_count, -1)


def pair_forward(pieces, segment, live_rows, query_block, head_scale):
    queries, keys_pair, values_pair = pieces
    row_count = queries.shape[0]
    head_width = queries.shape[1] // 2
    query_heads = queries.reshape(row_count, 2, head_width)
    key_heads = keys_pair.reshape(row_count, 2, head_width)
    value_heads = values_pair.reshape(row_count, 2, head_width)
    out_blocks = []
    total_blocks = []
    for row_start in range(0, row_count, query_block):
        allowed = allowed_block(segment, live_rows, row_start, query_block)
        scores = (
            jnp.einsum(
                "qhd,khd->hqk",
                query_heads[row_start : row_start + query_block],
                key_heads,
                preferred_element_type=jnp.float32,
            )
            * head_scale
        )
        scores = jnp.where(allowed, scores, masked_score)
        row_max = jnp.max(scores, axis=-1, keepdims=True)
        exp_scores = jnp.exp(scores - row_max)
        row_sum = jnp.sum(exp_scores, axis=-1, keepdims=True)
        attn_probs = (exp_scores / row_sum).astype(jnp.bfloat16)
        attended = jnp.einsum(
            "hqk,khd->qhd", attn_probs, value_heads, preferred_element_type=jnp.float32
        )
        out_blocks.append(attended.reshape(query_block, 2 * head_width))
        total_blocks.append((row_max + jnp.log(row_sum))[:, :, 0])
    return (jnp.concatenate(out_blocks, 0), jnp.concatenate(total_blocks, 1))


def pair_backward(pieces, segment, live_rows, query_block, head_scale):
    queries, keys_pair, values_pair, grad_pair, log_total = pieces
    row_count = queries.shape[0]
    head_width = queries.shape[1] // 2
    query_heads = queries.reshape(row_count, 2, head_width)
    key_heads = keys_pair.reshape(row_count, 2, head_width)
    value_heads = values_pair.reshape(row_count, 2, head_width)
    grad_heads = grad_pair.reshape(row_count, 2, head_width)
    grad_key = jnp.zeros((row_count, 2, head_width), jnp.float32)
    grad_value = jnp.zeros((row_count, 2, head_width), jnp.float32)
    query_grads = []
    for row_start in range(0, row_count, query_block):
        stop_row = row_start + query_block
        query_part = query_heads[row_start:stop_row]
        grad_part = grad_heads[row_start:stop_row]
        allowed = allowed_block(segment, live_rows, row_start, query_block)
        scores = (
            jnp.einsum("qhd,khd->hqk", query_part, key_heads, preferred_element_type=jnp.float32)
            * head_scale
        )
        scores = jnp.where(allowed, scores, masked_score)
        attn_probs = jnp.exp(scores - log_total[:, row_start:stop_row, None])
        grad_probs = jnp.einsum(
            "qhd,khd->hqk", grad_part, value_heads, preferred_element_type=jnp.float32
        )
        grad_scores = (
            attn_probs * (grad_probs - jnp.sum(grad_probs * attn_probs, axis=-1, keepdims=True))
        ).astype(jnp.bfloat16)
        query_grad = (
            jnp.einsum("hqk,khd->qhd", grad_scores, key_heads, preferred_element_type=jnp.float32)
            * head_scale
        )
        query_grads.append(query_grad.reshape(query_block, 2 * head_width))
        grad_key = (
            grad_key
            + jnp.einsum(
                "hqk,qhd->khd", grad_scores, query_part, preferred_element_type=jnp.float32
            )
            * head_scale
        )
        grad_value = grad_value + jnp.einsum(
            "hqk,qhd->khd",
            attn_probs.astype(jnp.bfloat16),
            grad_part,
            preferred_element_type=jnp.float32,
        )
    return (
        jnp.concatenate(query_grads, 0),
        grad_key.reshape(row_count, 2 * head_width),
        grad_value.reshape(row_count, 2 * head_width),
    )


def local(
    tokens,
    qkv_weight,
    out_weight,
    up_weight,
    down_weight,
    norm_gains,
    bias_rows,
    ff_bias,
    lengths,
    owners,
    cotangent,
):
    row_count, model_width = tokens.shape
    device = lax.axis_index("dp") * lax.axis_size("rep") + lax.axis_index("rep")
    segment, live_rows = token_segments(lengths, owners, device, row_count)
    query_block = min(512, row_count)
    head_pairs = HEADS // 2
    head_scale = HD ** (-0.5)
    layer_w = (
        lax.all_gather(qkv_weight, "dp", axis=0, tiled=True),
        lax.all_gather(out_weight, "dp", axis=0, tiled=True),
        lax.all_gather(up_weight, "dp", axis=0, tiled=True),
        lax.all_gather(down_weight, "dp", axis=0, tiled=True),
        lax.all_gather(norm_gains, "dp", axis=1, tiled=True),
        lax.all_gather(bias_rows, "dp", axis=1, tiled=True),
        lax.all_gather(ff_bias, "dp", axis=0, tiled=True),
    )
    w_qkv, w_out, w_up, w_down, gains_low, biases_low, up_bias_low = layer_w
    gain_rows = gains_low.astype(jnp.float32)
    shift_rows = biases_low.astype(jnp.float32)
    up_bias = up_bias_low.astype(jnp.float32)
    zero_bias = jnp.zeros((model_width,), jnp.float32)
    head_bias = jnp.concatenate([shift_rows[0], zero_bias, shift_rows[1]])
    projected = (jnp.dot(tokens, w_qkv, preferred_element_type=jnp.float32) + head_bias).astype(
        jnp.bfloat16
    )
    queries = split_pairs(projected[:, :model_width], head_pairs)
    keys_all = split_pairs(projected[:, model_width : 2 * model_width], head_pairs)
    values_all = split_pairs(projected[:, 2 * model_width :], head_pairs)

    def attend(pieces):
        return pair_forward(pieces, segment, live_rows, query_block, head_scale)

    mixed_pairs, log_total = lax.map(attend, (queries, keys_all, values_all))
    mixed_rows = join_pairs(mixed_pairs).astype(jnp.bfloat16)
    branch = jnp.dot(mixed_rows, w_out, preferred_element_type=jnp.float32) + shift_rows[2]
    first_norm, unit_one, inv_one = normalize_keep(
        tokens.astype(jnp.float32) + branch, gain_rows[0], shift_rows[4]
    )
    first_low = first_norm.astype(jnp.bfloat16)
    inner_pre = jnp.dot(first_low, w_up, preferred_element_type=jnp.float32) + up_bias
    activated, gelu_pull = jax.vjp(lambda values: jax.nn.gelu(values, approximate=False), inner_pre)
    hidden = activated.astype(jnp.bfloat16)
    ffn_out = jnp.dot(hidden, w_down, preferred_element_type=jnp.float32) + shift_rows[3]
    final_norm, unit_two, inv_two = normalize_keep(
        first_norm + ffn_out, gain_rows[1], shift_rows[5]
    )
    live_col = live_rows.astype(jnp.float32)[:, None]
    output = (final_norm * live_col).astype(jnp.bfloat16)
    gathered_again = (
        lax.all_gather(qkv_weight, "dp", axis=0, tiled=True),
        lax.all_gather(out_weight, "dp", axis=0, tiled=True),
        lax.all_gather(up_weight, "dp", axis=0, tiled=True),
        lax.all_gather(down_weight, "dp", axis=0, tiled=True),
        lax.all_gather(norm_gains, "dp", axis=1, tiled=True),
    )
    w_qkv, w_out, w_up, w_down, gains_again = gathered_again
    gain_rows = gains_again.astype(jnp.float32)
    grad_out = cotangent.astype(jnp.float32) * live_col
    d_gain_two = jnp.sum(grad_out * unit_two, axis=0)
    d_shift_two = jnp.sum(grad_out, axis=0)
    grad_two = normalize_back(grad_out, unit_two, inv_two, gain_rows[1])
    grad_ffn = grad_two.astype(jnp.bfloat16)
    d_down_bias = jnp.sum(grad_ffn.astype(jnp.float32), axis=0)
    d_down = jnp.einsum("tf,td->fd", hidden, grad_ffn, preferred_element_type=jnp.float32)
    grad_hidden = jnp.einsum("td,fd->tf", grad_ffn, w_down, preferred_element_type=jnp.float32)
    grad_inner = gelu_pull(grad_hidden)[0].astype(jnp.bfloat16)
    d_up_bias = jnp.sum(grad_inner.astype(jnp.float32), axis=0)
    d_up = jnp.einsum("td,tf->df", first_low, grad_inner, preferred_element_type=jnp.float32)
    grad_first = grad_two + jnp.einsum(
        "tf,df->td", grad_inner, w_up, preferred_element_type=jnp.float32
    )
    d_gain_one = jnp.sum(grad_first * unit_one, axis=0)
    d_shift_one = jnp.sum(grad_first, axis=0)
    grad_one = normalize_back(grad_first, unit_one, inv_one, gain_rows[0])
    grad_branch = grad_one.astype(jnp.bfloat16)
    d_out_bias = jnp.sum(grad_branch.astype(jnp.float32), axis=0)
    d_out = jnp.einsum("td,te->de", mixed_rows, grad_branch, preferred_element_type=jnp.float32)
    grad_mixed = jnp.einsum(
        "te,de->td", grad_branch, w_out, preferred_element_type=jnp.float32
    ).astype(jnp.bfloat16)

    def attend_back(pieces):
        return pair_backward(pieces, segment, live_rows, query_block, head_scale)

    grad_query, grad_key, grad_value = lax.map(
        attend_back, (queries, keys_all, values_all, split_pairs(grad_mixed, head_pairs), log_total)
    )
    grad_heads = jnp.concatenate(
        [join_pairs(grad_query), join_pairs(grad_key), join_pairs(grad_value)], 1
    ).astype(jnp.bfloat16)
    d_head_bias = jnp.sum(grad_heads.astype(jnp.float32), axis=0)
    d_qkv = jnp.einsum("td,te->de", tokens, grad_heads, preferred_element_type=jnp.float32)
    grad_tokens = grad_one + jnp.einsum(
        "te,de->td", grad_heads, w_qkv, preferred_element_type=jnp.float32
    )
    d_gains = jnp.stack([d_gain_one, d_gain_two])
    d_biases = jnp.stack(
        [
            d_head_bias[:model_width],
            d_head_bias[2 * model_width :],
            d_out_bias,
            d_down_bias,
            d_shift_one,
            d_shift_two,
        ]
    )
    column_parts = (
        lax.psum_scatter(d_qkv.astype(jnp.bfloat16), "rep", scatter_dimension=1, tiled=True).astype(
            jnp.float32
        ),
        lax.psum_scatter(d_out.astype(jnp.bfloat16), "rep", scatter_dimension=1, tiled=True).astype(
            jnp.float32
        ),
        lax.psum_scatter(d_up.astype(jnp.bfloat16), "rep", scatter_dimension=1, tiled=True).astype(
            jnp.float32
        ),
        lax.psum_scatter(
            d_down.astype(jnp.bfloat16), "rep", scatter_dimension=1, tiled=True
        ).astype(jnp.float32),
    )
    owned = (
        lax.psum_scatter(column_parts[0], "dp", scatter_dimension=0, tiled=True),
        lax.psum_scatter(column_parts[1], "dp", scatter_dimension=0, tiled=True),
        lax.psum_scatter(column_parts[2], "dp", scatter_dimension=0, tiled=True),
        lax.psum_scatter(column_parts[3], "dp", scatter_dimension=0, tiled=True),
        lax.psum_scatter(d_gains, "dp", scatter_dimension=1, tiled=True),
        lax.psum_scatter(d_biases, "dp", scatter_dimension=1, tiled=True),
        lax.psum_scatter(d_up_bias, "dp", scatter_dimension=0, tiled=True),
    )
    small_sums = lax.psum((owned[4], owned[5], owned[6]), "rep")
    full_rows = (
        lax.all_gather(owned[0].astype(jnp.bfloat16), "rep", axis=1, tiled=True).astype(
            jnp.float32
        ),
        lax.all_gather(owned[1].astype(jnp.bfloat16), "rep", axis=1, tiled=True).astype(
            jnp.float32
        ),
        lax.all_gather(owned[2].astype(jnp.bfloat16), "rep", axis=1, tiled=True).astype(
            jnp.float32
        ),
        lax.all_gather(owned[3].astype(jnp.bfloat16), "rep", axis=1, tiled=True).astype(
            jnp.float32
        ),
    )
    return (
        output,
        grad_tokens,
        full_rows[0],
        full_rows[1],
        full_rows[2],
        full_rows[3],
        small_sums[0],
        small_sums[1],
        small_sums[2],
    )


def solution(mesh):
    in_specs = (
        P(("dp", "rep"), None),
        P("dp", None),
        P("dp", None),
        P("dp", None),
        P("dp", None),
        P(None, "dp"),
        P(None, "dp"),
        P("dp"),
        P(),
        P(),
        P(("dp", "rep"), None),
    )
    out_specs = (
        P(("dp", "rep"), None),
        P(("dp", "rep"), None),
        P("dp", None),
        P("dp", None),
        P("dp", None),
        P("dp", None),
        P(None, "dp"),
        P(None, "dp"),
        P("dp"),
    )
    return jax.shard_map(local, mesh=mesh, in_specs=in_specs, out_specs=out_specs, check_vma=False)
```

profile of v0, /device:TPU:0, one launch (start us, length us, event | category | flops | bytes accessed | tf_op | source)
XLA Modules:
  0.0 1022.6 jit_solution(13829500621667868581)
XLA Ops:
  14.6 3.7 scatter_custom_fusion
  18.8 28.6 %all-gather = bf16[8,96,6]{1,2,0:T(8,128)(2,1)S(1)} all-gather(bf16[1,96,6]{1,2,0:T(8,128)(2,1)} %bitcast.284), channel_id=1, replica_groups=mesh['dp'=8,'rep'=4] {'dp'}, dimensions={0}, use_global_device_ids=true | all-gather | bytes 10368 | tf_op jit(solution)/shard_map/all_gather | solution.py:176
  48.2 2.6 copy.79
  50.8 19.7 %all-gather.1 = bf16[8,96,2]{1,2,0:T(2,128)(2,1)S(1)} all-gather(bf16[1,96,2]{1,2,0:T(2,128)(2,1)S(1)} %bitcast.285), channel_id=1, replica_groups=mesh['dp'=8,'rep'=4] {'dp'}, dimensions={0}, use_global_device_ids=true | all-gather | bytes 3456 | tf_op jit(solution)/shard_map/all_gather | solution.py:175
  71.2 26.1 %all-gather.2 = bf16[8,1,384]{2,1,0:T(2,128)(2,1)S(1)} all-gather(bf16[1,1,384]{2,1,0:T(2,128)(2,1)S(1)} %reshape.491), channel_id=1, replica_groups=mesh['dp'=8,'rep'=4] {'dp'}, dimensions={0}, use_global_device_ids=true | all-gather | bytes 6912 | tf_op jit(solution)/shard_map/all_gather | solution.py:177
  97.3 1.8 copy.86
  99.2 6.0 add_convert_fusion.1
  105.2 2.0 fusion.60
  107.2 1.7 copy.81
  108.9 2.6 copy.82
  111.5 1.6 copy.83
  114.5 74.6 %while.26 = (s32[]{:T(128)}, bf16[6,1024,128]{1,2,0:T(8,128)(2,1)}, f32[6,2,1024]{2,1,0:T(2,128)}, bf16[6,1024,128]{1,2,0:T(8,128)(2,1)S(1)}, s32[1024]{0:T(1024...) while((s32[]{:T(128)}, bf16[6,1024,128]{1,2,0:T(8,128)(2,1)}, ...), condition=%wide.region_10.11_spmd, body=%wide.region_5.10_spmd.sunk | while | flops 567804416 | bytes 33137796 | solution.py:195
  114.5 1.6 fusion.165
  126.9 1.6 fusion.165
  164.2 1.6 fusion.165
  190.1 3.8 fusion.62
  194.4 5.9 all-gather.13.cloned.1.call-done
  200.3 37.7 %multiply_convert_fusion.2 = (bf16[1024,3072]{1,0:T(8,128)(2,1)}, f32[1024,3072]{1,0:T(8,128)}, f32[1024,3072]{1,0:T(8,128)}) fusion(f32[3072]{0:T(1024)S(1)} %bitcast.282, bf16[768,3072]{1,0:T(8,128)(2,1)} %all-gather.13.cloned.1.call-done, f32[1024,768]{0,1:T(8,128)S(1)} %get-tuple-element.266, f32[768]{0:T(1024)S(1)} %get-tuple-element.171, ...), kind=kOutput, calls=%fused_computation.73 | convolution fusion | flops 5043388416 | bytes 39348224 | tf_op jit(solution)/shard_map/dot_general | solution.py:202
  238.1 42.0 %all-gather.15.cloned.1.call-done = bf16[3072,768]{1,0:T(8,128)(2,1)} async-done(((bf16[384,768]{1,0:T(8,128)(2,1)}), bf16[3072,768]{1,0:T(8,128)(2,1)}) %all-gather.15.cloned.1.call-update) | async-done | bytes 4718608 | tf_op jit(solution)/shard_map/all_gather | solution.py:174
  280.1 9.4 fusion.63
  290.9 2.1 multiply_reduce_fusion.2
  293.0 3.4 convert_reduce_fusion.2
  296.4 18.1 %convert_reduce_fusion = (f32[3072]{0:T(1024)}, bf16[1024,3072]{1,0:T(8,128)(2,1)}) fusion(f32[1024,3072]{1,0:T(8,128)} %get-tuple-element.223, bf16[1024,768]{0,1:T(8,128)(2,1)S(1)} %get-tuple-element.219, bf16[3072,768]{1,0:T(8,128)(2,1)} %all-gather.15.cloned.1.call-done, f32[1024,3072]{1,0:T(8,128)} %get-tuple-element.267, f32[3072]{0:T(1024)S(1)} %bitcast.283), kind=kOutput, calls=%fused_computation.71 | convolution fusion | flops 4885312512 | bytes 37773312 | tf_op jit(solution)/shard_map/td,fd->tf/dot_general | solution.py:227
  314.5 11.2 %multiply_reduce_fusion.3 = (f32[768]{0:T(1024)S(1)}, f32[1024]{0:T(1024)S(1)}, f32[1024]{0:T(1024)S(1)}, f32[768]{0:T(1024)S(1)}, f32[1024,768]{0,1:T(8,128)S(1)}) fusion(f32[1024,768]{0,1:T(8,128)} %copy-done.1, f32[1024]{0:T(1024)S(1)} %add_rsqrt_fusion.1, f32[1024]{0:T(1024)S(1)} %broadcast_multiply_fusion.5, f32[768]{0:T(1024)S(1)} %get-tuple-element.176, ...), kind=kOutput, calls=%fused_computation.97 | convolution fusion | flops 4846776320 | bytes 22069248 | tf_op jit(solution)/shard_map/tf,df->td/dot_general | solution.py:231
  326.9 5.0 convolution_convert_fusion.4
  331.9 3.8 convolution_convert_fusion.3
  337.5 120.0 %while.27 = (s32[]{:T(128)}, bf16[6,1024,128]{1,2,0:T(8,128)(2,1)S(1)}, bf16[6,1024,128]{1,2,0:T(8,128)(2,1)S(1)}, bf16[6,1024,128]{1,2,0:T(8,128)(2,1)}, bf16[6...) while((s32[]{:T(128)}, ...), condition=%wide.region_22.23_spmd, body=%wide.region_19.22_spmd.sunk | while | flops 1380317696 | bytes 76382888 | solution.py:247
  344.8 1.8 multiply_reduce_fusion.12
  349.1 1.8 multiply_reduce_fusion.11
  360.4 1.6 fusion.198
  364.7 1.8 multiply_reduce_fusion.12
  369.0 1.8 multiply_reduce_fusion.11
  384.6 1.8 multiply_reduce_fusion.12
  388.9 1.8 multiply_reduce_fusion.11
  404.5 1.8 multiply_reduce_fusion.12
  408.8 1.8 multiply_reduce_fusion.11
  424.4 1.8 multiply_reduce_fusion.12
  428.8 1.8 multiply_reduce_fusion.11
  444.4 1.8 multiply_reduce_fusion.12
  448.7 1.8 multiply_reduce_fusion.11
  457.5 8.6 fusion.39
  466.2 9.0 convolution_convert_fusion
  475.4 1.8 copy-done.3
  477.2 9.8 convolution_convert_fusion.1
  489.0 1.9 convert_reduce_fusion.1
  492.2 2.0 copy.100
  494.3 10.9 %reduce-scatter.19.cloned.1.call-done = bf16[768,576]{0,1:T(8,128)(2,1)} async-done(((bf16[768,2304]{0,1:T(8,128)(2,1)}), bf16[768,576]{0,1:T(8,128)(2,1)}) %reduce-scatter.19.cloned.1.call-update) | async-done | bytes 884752 | tf_op jit(solution)/shard_map/reduce_scatter | solution.py:270
  505.1 2.5 copy.98
  507.7 48.0 %reduce-scatter.27.cloned.1.call-done = bf16[3072,192]{0,1:T(8,128)(2,1)} async-done(((bf16[3072,768]{0,1:T(8,128)(2,1)}), bf16[3072,192]{0,1:T(8,128)(2,1)}) %reduce-scatter.27.cloned.1.call-update) | async-done | bytes 1179664 | tf_op jit(solution)/shard_map/reduce_scatter | solution.py:279
  555.7 50.3 %reduce-scatter.23.cloned.1.call-done = bf16[768,768]{1,0:T(8,128)(2,1)} async-done(((bf16[768,3072]{1,0:T(8,128)(2,1)}), bf16[768,768]{1,0:T(8,128)(2,1)}) %reduce-scatter.23.cloned.1.call-update) | async-done | bytes 1179664 | tf_op jit(solution)/shard_map/reduce_scatter | solution.py:276
  607.3 8.9 convolution_add_fusion.2
  616.2 3.7 copy.92
  621.4 37.5 %all-reduce.1 = f32[3072]{0:T(1024)S(1)} all-reduce(f32[3072]{0:T(1024)S(1)} %copy-done.24), channel_id=12, replica_groups=mesh['dp'=8,'rep'=4] {'dp'}, use_global_device_ids=true, to_apply=%region_43.44.clone | all-reduce | flops 3072 | bytes 24576
  659.0 13.0 %reduce-scatter.35.cloned.1.call-done = f32[96,2]{1,0:T(8,128)} async-done(((f32[768,2]{1,0:T(8,128)}), f32[96,2]{1,0:T(8,128)}) %reduce-scatter.35.cloned.1.call-update) | async-done | bytes 784
  672.9 63.5 %reduce-scatter.37.cloned.1.call-done = f32[96,6]{1,0:T(8,128)} async-done(((f32[768,6]{1,0:T(8,128)}), f32[96,6]{1,0:T(8,128)}) %reduce-scatter.37.cloned.1.call-update) | async-done | bytes 2320
  737.2 6.3 all-reduce.2
  743.5 59.1 %reduce-scatter.33.cloned.1.call-done = f32[96,192]{1,0:T(8,128)} async-done(((f32[768,192]{1,0:T(8,128)}), f32[96,192]{1,0:T(8,128)}) %reduce-scatter.33.cloned.1.call-update) | async-done | bytes 73744
  803.6 5.6 all_gather.46
  810.1 62.6 %reduce-scatter.31.cloned.1.call-done = f32[96,576]{1,0:T(8,128)} async-done(((f32[768,576]{1,0:T(8,128)}), f32[96,576]{1,0:T(8,128)}) %reduce-scatter.31.cloned.1.call-update) | async-done | bytes 221200
  873.9 6.9 all-gather.3
  882.6 57.2 %reduce-scatter.29.cloned.1.call-done = bf16[384,192]{0,1:T(8,128)(2,1)} async-done(((bf16[3072,192]{0,1:T(8,128)(2,1)}), bf16[384,192]{0,1:T(8,128)(2,1)}) %reduce-scatter.29.cloned.1.call-update) | async-done | bytes 147472 | tf_op jit(solution)/shard_map/reduce_scatter | solution.py:287
  939.8 7.7 all_gather.48
  948.8 58.2 %reduce-scatter.25.cloned.1.call-done = bf16[96,768]{1,0:T(8,128)(2,1)} async-done(((bf16[768,768]{1,0:T(8,128)(2,1)}), bf16[96,768]{1,0:T(8,128)(2,1)}) %reduce-scatter.25.cloned.1.call-update) | async-done | bytes 147472 | tf_op jit(solution)/shard_map/reduce_scatter | solution.py:286
  1007.0 7.6 all_gather.47
  (379 shorter events, 196.9 us)
Async XLA Ops:
  7.2 92.0 %copy-start.14 = (bf16[1024,768]{1,0:T(8,128)(2,1)S(1)}, bf16[1024,768]{1,0:T(8,128)(2,1)}, u32[]{:S(2)}) copy-start(bf16[1024,768]{1,0:T(8,128)(2,1)} %param.15) | copy-start | bytes 4718596
  7.2 43.6 %copy-start.29 = (bf16[2,96]{1,0:T(2,128)(2,1)S(1)}, bf16[2,96]{1,0:T(2,128)(2,1)}, u32[]{:S(2)}) copy-start(bf16[2,96]{1,0:T(2,128)(2,1)} %param.20) | copy-start | bytes 1156
  7.2 64.0 %copy-start.28 = (bf16[384]{0:T(512)(128)(2,1)S(1)}, bf16[384]{0:T(512)(128)(2,1)}, u32[]{:S(2)}) copy-start(bf16[384]{0:T(512)(128)(2,1)} %param.22) | copy-start | bytes 2308
  7.2 90.1 %copy-start.13 = (bf16[1024,768]{1,0:T(8,128)(2,1)S(1)}, bf16[1024,768]{1,0:T(8,128)(2,1)}, u32[]{:S(2)}) copy-start(bf16[1024,768]{1,0:T(8,128)(2,1)} %param.25) | copy-start | bytes 4718596
  7.2 91.9 %all-gather.9.cloned.1.call-start = ((), (), s32[]{:S(2)}) async-start(), calls=%async_computation.10 | async-start | bytes 3981312 | tf_op jit(solution)/shard_map/all_gather | solution.py:171
  8.0 181.1 %all-gather.11.cloned.1.call-start = ((), (), s32[]{:S(2)}) async-start(), calls=%async_computation.11 | async-start | bytes 1327104 | tf_op jit(solution)/shard_map/all_gather | solution.py:172
  8.7 191.6 %all-gather.13.cloned.1.call-start = ((), (), s32[]{:S(2)}) async-start(), calls=%async_computation.12 | async-start | bytes 5308416 | tf_op jit(solution)/shard_map/all_gather | solution.py:173
  9.4 270.7 %all-gather.15.cloned.1.call-start = ((), (), s32[]{:S(2)}) async-start(), calls=%async_computation.13 | async-start | bytes 5308416 | tf_op jit(solution)/shard_map/all_gather | solution.py:174
  10.0 482.1 %reduce-scatter.21.cloned.1.call-start = ((), (), s32[]{:S(2)}) async-start(), calls=%async_computation.15 | async-start | bytes 1474560 | tf_op jit(solution)/shard_map/reduce_scatter | solution.py:273
  48.2 231.9 %copy-start.25 = (f32[768]{0:T(1024)}, f32[768]{0:T(1024)S(1)}, u32[]{:S(2)}) copy-start(f32[768]{0:T(1024)S(1)} %get-tuple-element.171) | copy-start | bytes 9220
  189.0 1.1 copy-start.4
  189.0 5.0 copy-start.11
  189.0 5.0 copy-start.16
  194.0 86.1 %copy-start.1 = (f32[1024,768]{0,1:T(8,128)}, f32[1024,768]{0,1:T(8,128)S(1)}, u32[]{:S(2)}) copy-start(f32[1024,768]{0,1:T(8,128)S(1)} %get-tuple-element.266) | copy-start | bytes 9437188
  200.3 79.8 %copy-start.27 = (f32[768]{0:T(1024)S(1)}, f32[768]{0:T(1024)}, u32[]{:S(2)}) copy-start(f32[768]{0:T(1024)} %get-tuple-element.170) | copy-start | bytes 9220
  280.1 9.8 copy-start.18
  280.1 9.8 copy-start.19
  289.5 1.4 copy-start
  289.5 3.5 copy-start.23
  296.4 18.1 %copy-start.15 = (bf16[1024,768]{0,1:T(8,128)(2,1)}, bf16[1024,768]{0,1:T(8,128)(2,1)S(1)}, u32[]{:S(2)}) copy-start(bf16[1024,768]{0,1:T(8,128)(2,1)S(1)} %get-tuple-element.219) | copy-start | bytes 4718596
  314.5 11.2 %copy-start.2 = (f32[1024,768]{0,1:T(8,128)S(1)}, f32[1024,768]{0,1:T(8,128)}, u32[]{:S(2)}) copy-start(f32[1024,768]{0,1:T(8,128)} %copy-done.1) | copy-start | bytes 9437188
  326.9 5.1 copy-start.10
  331.9 173.2 %reduce-scatter.19.cloned.1.call-start = ((), (), s32[]{:S(2)}) async-start(), calls=%async_computation.14 | async-start | bytes 4423680 | tf_op jit(solution)/shard_map/reduce_scatter | solution.py:270
  335.7 1.8 copy-start.12
  335.7 1.8 copy-start.17
  457.5 8.6 copy-start.5
  457.5 8.6 copy-start.7
  466.2 89.4 %reduce-scatter.27.cloned.1.call-start = ((), (), s32[]{:S(2)}) async-start(), calls=%async_computation.18 | async-start | bytes 5898240 | tf_op jit(solution)/shard_map/reduce_scatter | solution.py:279
  475.3 1.9 copy-start.3
  475.3 1.9 copy-start.26
  475.3 130.7 %reduce-scatter.23.cloned.1.call-start = ((), (), s32[]{:S(2)}) async-start(), calls=%async_computation.16 | async-start | bytes 5898240 | tf_op jit(solution)/shard_map/reduce_scatter | solution.py:276
  487.0 0.7 copy-start.22
  487.0 1.6 copy-start.6
  487.0 2.0 copy-start.8
  487.0 4.1 copy-start.21
  487.0 4.1 copy-start.20
  487.0 185.0 %reduce-scatter.35.cloned.1.call-start = ((), (), s32[]{:S(2)}) async-start(), calls=%async_computation.22 | async-start | bytes 442368
  490.9 245.4 %reduce-scatter.37.cloned.1.call-start = ((), (), s32[]{:S(2)}) async-start(), calls=%async_computation.23 | async-start | bytes 442368
  492.1 310.5 %reduce-scatter.33.cloned.1.call-start = ((), (), s32[]{:S(2)}) async-start(), calls=%async_computation.21 | async-start | bytes 884736
  494.2 111.9 %copy-start.30 = (u32[32]{0:T(128)S(1)}, u32[32]{0:T(128)}, u32[]{:S(2)}) copy-start(u32[32]{0:T(128)} %constant.156) | copy-start | bytes 388
  494.2 378.4 %reduce-scatter.31.cloned.1.call-start = ((), (), s32[]{:S(2)}) async-start(), calls=%async_computation.20 | async-start | bytes 2211840
  507.6 432.2 %reduce-scatter.29.cloned.1.call-start = ((), (), s32[]{:S(2)}) async-start(), calls=%async_computation.19 | async-start | bytes 1327104 | tf_op jit(solution)/shard_map/reduce_scatter | solution.py:287
  555.7 451.4 %reduce-scatter.25.cloned.1.call-start = ((), (), s32[]{:S(2)}) async-start(), calls=%async_computation.17 | async-start | bytes 1327104 | tf_op jit(solution)/shard_map/reduce_scatter | solution.py:286
  616.2 3.7 copy-start.9
  616.2 5.2 copy-start.24
Sparse Core Ops, SparseCore 0:
  10.2 67.6 all-gather.8
  80.1 39.9 all-gather.10
  122.3 78.0 all-gather.12
  202.4 77.6 all-gather.14
  332.0 23.9 reduce-scatter.20
  466.3 38.7 reduce-scatter.18
  507.7 47.9 reduce-scatter.26
  558.2 47.7 reduce-scatter.22
  609.8 62.1 reduce-scatter.34
  675.1 61.1 reduce-scatter.36
  740.2 62.3 reduce-scatter.32
  805.9 66.6 reduce-scatter.30
  876.0 63.7 reduce-scatter.28
  943.1 63.9 reduce-scatter.24
where the time goes:
time: 1030 us; the launch traced here: 1020 us
  waiting for transfers between devices  473 us (46%)
  matrix products  223 us (22%)
  blocking collectives  146 us (14%)
  local copies, waits for them, and re-layouts  83 us (8%)
  other arithmetic  79.7 us (8%)
  between operations  15.4 us (1%)
    unnamed x18, waiting for transfers between devices  201 us
    reduce_scatter x1, waiting for transfers between devices, local(): lax.psum_scatter(column_parts[2], 'dp', scatter_dimension=0, tiled=True)  58.2 us
    reduce_scatter x1, waiting for transfers between devices, local(): lax.psum_scatter(column_parts[3], 'dp', scatter_dimension=0, tiled=True)  57.2 us
    reduce_scatter x1, waiting for transfers between devices, local(): lax.psum_scatter(d_up.astype(jnp.bfloat16), 'rep', scatter_dimension=1, t...  50.3 us
    reduce_scatter x1, waiting for transfers between devices, local(): lax.psum_scatter(d_down.astype(jnp.bfloat16), 'rep', scatter_dimension=1,...  48 us
    all_gather x1, waiting for transfers between devices, local(): lax.all_gather(down_weight, 'dp', axis=0, tiled=True)  42 us
    dot_general x1, matrix products, local(): jnp.dot(first_low, w_up, preferred_element_type=jnp.float32) + up_bias  37.7 us
    unnamed x1, blocking collectives  37.5 us
  transfers between devices with their start and end apart: 14, of which 11 were waited for; matrix products, arithmetic and copies ran while one was open for 32% of the time, Pallas kernels for 0%

commit v1 on v0

--- a/solution.py
+++ b/solution.py
@@ -1,14 +1,353 @@
+import functools
+
 import jax
 import jax.numpy as jnp
 from jax import lax
+from jax.experimental import pallas as pl
+from jax.experimental.pallas import tpu as pltpu
 from jax.sharding import PartitionSpec as P
 
 HEADS = 12
 HD = 64
-
-
+LONG = 512
+SHORT = 64
 norm_eps = 1e-06
 masked_score = -1000000000.0
+BF = jnp.bfloat16
+F32 = jnp.float32
+VMEM_LIMIT = 62 * 1024 * 1024
+
+NN = (((1,), (0,)), ((), ()))
+NT = (((1,), (1,)), ((), ()))
+TN = (((0,), (0,)), ((), ()))
+
+
+def dot(a, b, dims=NN):
+    return lax.dot_general(a, b, dims, preferred_element_type=F32)
+
+
+def vm():
+    return pl.BlockSpec(memory_space=pltpu.VMEM)
+
+
+def sm():
+    return pl.BlockSpec(memory_space=pltpu.SMEM)
+
+
+def params(**kw):
+    return pltpu.CompilerParams(vmem_limit_bytes=VMEM_LIMIT, **kw)
+
+
+def place_of():
+    dp, rep = lax.axis_index("dp"), lax.axis_index("rep")
+    return dp // 2, dp % 2, rep // 2, rep % 2
+
+
+def peers(z, y, x, c):
+    def at(z2, y2, x2, c2):
+        return (z2 * 2 + y2, x2 * 2 + c2)
+
+    return (
+        [at((z + k) % 4, y, x, c) for k in (1, 2, 3)],
+        at(z, 1 - y, x, c),
+        at(z, y, 1 - x, c),
+        at(z, y, x, 1 - c),
+    )
+
+
+def greet(zs, yp, xp, cp):
+    barrier = pltpu.get_barrier_semaphore()
+    for peer in (*zs, yp, xp, cp):
+        pl.semaphore_signal(barrier, inc=1, device_id=peer, device_id_type=pl.DeviceIdType.MESH)
+    pl.semaphore_wait(barrier, 6)
+
+
+def remote(src, dst, ssem, rsem, peer):
+    return pltpu.make_async_remote_copy(
+        src_ref=src, dst_ref=dst, send_sem=ssem, recv_sem=rsem,
+        device_id=peer, device_id_type=pl.DeviceIdType.MESH,
+    )
+
+
+def wavefront(count, stages):
+    for t in range(count + len(stages) - 1):
+        for s in range(len(stages) - 1, -1, -1):
+            if 0 <= t - s < count:
+                stages[s](t - s)
+
+
+def gather_kernel(n, *refs):
+    shards, fulls = refs[:n], refs[n : 2 * n]
+    ssem, rsem, lsem = refs[2 * n :]
+    z, y, x, c = place_of()
+    zs, yp, xp, cp = peers(z, y, x, c)
+    greet(zs, yp, xp, cp)
+    sent = []
+
+    def go(w, i, src, dst, peer):
+        copy = remote(src, dst, ssem.at[w, i], rsem.at[w, i], peer)
+        copy.start()
+        sent.append(copy)
+
+    def arrive(w, i, ref):
+        remote(ref, ref, ssem.at[w, i], rsem.at[w, i], cp).wait_recv()
+
+    def local(w):
+        return pltpu.make_async_copy(shards[w], fulls[w].at[z, y], lsem.at[w])
+
+    def near(w):
+        local(w).start()
+        src = shards[w].at[c, pl.ds(x, 2)]
+        dst = fulls[w].at[z, y, c, pl.ds(x, 2)]
+        for k in range(3):
+            go(w, k, src, dst, zs[k])
+        go(w, 3, src, dst, yp)
+
+    def mid(w):
+        for k in range(3):
+            zk = (z + 3 - k) % 4
+            part = fulls[w].at[zk, y, c, pl.ds(x, 2)]
+            arrive(w, k, part)
+            go(w, 4 + k, part, part, yp)
+            q = fulls[w].at[zk, y, c, 2 * x]
+            go(w, 7 + k, q, q, xp)
+
+    def far(w):
+        for k in range(4):
+            zk = (z + 4 - k) % 4
+            part = fulls[w].at[zk, 1 - y, c, pl.ds(x, 2)]
+            arrive(w, 3 + k, part)
+            q = fulls[w].at[zk, 1 - y, c, 2 * x]
+            go(w, 10 + k, q, q, xp)
+
+    def across(w):
+        for k in range(7):
+            zk, yk = ((z + 3 - k) % 4, y) if k < 3 else ((z + 7 - k) % 4, 1 - y)
+            arrive(w, 7 + k, fulls[w].at[zk, yk, c, 2 * (1 - x)])
+            half = fulls[w].at[zk, yk, c]
+            go(w, 14 + k, half, half, cp)
+
+    def last(w):
+        for k in range(7):
+            zk, yk = ((z + 3 - k) % 4, y) if k < 3 else ((z + 7 - k) % 4, 1 - y)
+            arrive(w, 14 + k, fulls[w].at[zk, yk, 1 - c])
+        local(w).wait()
+
+    wavefront(n, [near, mid, far, across, last])
+    for copy in sent:
+        copy.wait_send()
+
+
+def blocks(shard):
+    rows, columns = shard.shape
+    return shard.reshape(2, 3, rows // 6, columns)
+
+
+def gather(shards):
+    n = len(shards)
+    views = [blocks(s) for s in shards]
+    fulls = pl.pallas_call(
+        functools.partial(gather_kernel, n),
+        out_shape=[jax.ShapeDtypeStruct((4, 2) + v.shape, v.dtype) for v in views],
+        in_specs=[vm()] * n,
+        out_specs=[pl.BlockSpec(memory_space=pl.ANY)] * n,
+        scratch_shapes=[
+            pltpu.SemaphoreType.DMA((n, 21)),
+            pltpu.SemaphoreType.DMA((n, 21)),
+            pltpu.SemaphoreType.DMA((n,)),
+        ],
+        compiler_params=params(collective_id=0, has_side_effects=True),
+        name="gather",
+    )(*views)
+    return [f.reshape(8 * s.shape[0], s.shape[1]) for f, s in zip(fulls, shards)]
+
+
+def scatter_kernel(n, *refs):
+    grads, outs = refs[:n], refs[n : 2 * n]
+    half, rx, rpy, rqy, rpz, rqz, rpx, fin, got = (refs[(2 + i) * n : (3 + i) * n] for i in range(9))
+    ssem, rsem = refs[11 * n :]
+    z, y, x, c = place_of()
+    zs, yp, xp, cp = peers(z, y, x, c)
+    greet(zs, yp, xp, cp)
+    sent = []
+
+    def go(w, i, src, dst, peer):
+        copy = remote(src, dst, ssem.at[w, i], rsem.at[w, i], peer)
+        copy.start()
+        sent.append(copy)
+
+    def arrive(w, i, ref):
+        remote(ref, ref, ssem.at[w, i], rsem.at[w, i], cp).wait_recv()
+
+    def add(*parts):
+        total = parts[0].astype(F32)
+        for part in parts[1:]:
+            total = total + part.astype(F32)
+        return total
+
+    def s0(w):
+        go(w, 0, grads[w].at[:, :, 1 - c], half[w], cp)
+
+    def s1(w):
+        arrive(w, 0, half[w])
+        a = half[w]
+
+        @pl.loop(0, 4)
+        def _(i):
+            for j in range(2):
+                for k in range(3):
+                    a[i, j, k] = add(grads[w][i, j, c, k], a[i, j, k]).astype(a.dtype)
+
+        go(w, 1, a.at[:, :, 2 * (1 - x)], rx[w], xp)
+        go(w, 2, a.at[:, 1 - y, 1], rpy[w], yp)
+
+    def s2(w):
+        a = half[w]
+        arrive(w, 2, rpy[w])
+
+        @pl.loop(0, 4)
+        def _(i):
+            a[i, y, 1] = add(a[i, y, 1], rpy[w][i]).astype(a.dtype)
+
+        for k in range(3):
+            go(w, 3 + k, a.at[(z + k + 1) % 4, y, 1], rpz[w].at[k], zs[k])
+        arrive(w, 1, rx[w])
+
+        @pl.loop(0, 4)
+        def _(i):
+            for j in range(2):
+                a[i, j, 2 * x] = add(a[i, j, 2 * x], rx[w][i, j]).astype(a.dtype)
+
+        go(w, 6, a.at[:, 1 - y, 2 * x], rqy[w], yp)
+
+    def s3(w):
+        a = half[w]
+        arrive(w, 6, rqy[w])
+
+        @pl.loop(0, 4)
+        def _(i):
+            a[i, y, 2 * x] = add(a[i, y, 2 * x], rqy[w][i]).astype(a.dtype)
+
+        for k in range(3):
+            go(w, 7 + k, a.at[(z + k + 1) % 4, y, 2 * x], rqz[w].at[k], zs[k])
+        for k in range(3):
+            arrive(w, 3 + k, rpz[w].at[k])
+        a[z, y, 1] = add(a[z, y, 1], rpz[w][0], rpz[w][1], rpz[w][2]).astype(a.dtype)
+        go(w, 10, a.at[z, y, 1], rpx[w], xp)
+
+    def s4(w):
+        a = half[w]
+        for k in range(3):
+            arrive(w, 7 + k, rqz[w].at[k])
+        fin[w][0] = add(a[z, y, 2 * x], rqz[w][0], rqz[w][1], rqz[w][2]).astype(a.dtype)
+        go(w, 11, fin[w].at[0], got[w].at[c, 2 * x], xp)
+        go(w, 13, fin[w].at[0], got[w].at[c, 2 * x], cp)
+        arrive(w, 10, rpx[w])
+        fin[w][1] = add(a[z, y, 1], rpx[w][...]).astype(a.dtype)
+        go(w, 14, fin[w].at[1], got[w].at[c, 1], cp)
+
+    def s5(w):
+        arrive(w, 11, got[w].at[c, 2 * (1 - x)])
+        piece = got[w].at[c, 2 * (1 - x)]
+        go(w, 12, piece, piece, cp)
+        outs[w][c, 2 * x] = fin[w][0].astype(F32)
+        outs[w][c, 1] = fin[w][1].astype(F32)
+        outs[w][c, 2 * (1 - x)] = got[w][c, 2 * (1 - x)].astype(F32)
+
+    def s6(w):
+        arrive(w, 12, got[w].at[1 - c, 2 * (1 - x)])
+        arrive(w, 13, got[w].at[1 - c, 2 * x])
+        arrive(w, 14, got[w].at[1 - c, 1])
+        for k in range(3):
+            outs[w][1 - c, k] = got[w][1 - c, k].astype(F32)
+
+    wavefront(n, [s0, s1, s2, s3, s4, s5, s6])
+    for copy in sent:
+        copy.wait_send()
+
+
+def scatter(grads):
+    n = len(grads)
+    views = [g.reshape(4, 2, 2, 3, g.shape[0] // 48, g.shape[1]) for g in grads]
+    lead = ((4, 2, 3), (4, 2), (4,), (4,), (3,), (3,), (), (2,), (2, 3))
+    scratch = [pltpu.VMEM(s + v.shape[4:], v.dtype) for s in lead for v in views]
+    outs = pl.pallas_call(
+        functools.partial(scatter_kernel, n),
+        out_shape=[jax.ShapeDtypeStruct(v.shape[2:], F32) for v in views],
+        in_specs=[vm()] * n,
+        out_specs=[vm()] * n,
+        scratch_shapes=scratch
+        + [pltpu.SemaphoreType.DMA((n, 15)), pltpu.SemaphoreType.DMA((n, 15))],
+        compiler_params=params(collective_id=1, has_side_effects=True),
+        name="scatter",
+    )(*views)
+    return [o.reshape(g.shape[0] // 8, g.shape[1]) for o, g in zip(outs, grads)]
+
+
+def square():
+    return lax.axis_size("dp") == 8 and lax.axis_size("rep") == 4
+
+
+def gather_layer(qkv_weight, out_weight, up_weight, down_weight, norm_gains, bias_rows, ff_bias):
+    if not square():
+        return (
+            lax.all_gather(qkv_weight, "dp", axis=0, tiled=True),
+            lax.all_gather(out_weight, "dp", axis=0, tiled=True),
+            lax.all_gather(up_weight, "dp", axis=0, tiled=True),
+            lax.all_gather(down_weight, "dp", axis=0, tiled=True),
+            lax.all_gather(norm_gains, "dp", axis=1, tiled=True),
+            lax.all_gather(bias_rows, "dp", axis=1, tiled=True),
+            lax.all_gather(ff_bias, "dp", axis=0, tiled=True),
+        )
+    small = jnp.concatenate([bias_rows.reshape(-1), norm_gains.reshape(-1), ff_bias])
+    used = small.shape[0]
+    small = jnp.pad(small, (0, 96 * 128 - used)).reshape(96, 128)
+    full = gather([small, qkv_weight, out_weight, up_weight, down_weight])
+    rows = full[0].reshape(8, 96 * 128)[:, :used]
+    nb, ng = bias_rows.size, norm_gains.size
+    biases = rows[:, :nb].reshape(8, bias_rows.shape[0], -1).transpose(1, 0, 2)
+    gains = rows[:, nb : nb + ng].reshape(8, norm_gains.shape[0], -1).transpose(1, 0, 2)
+    return (
+        full[1], full[2], full[3], full[4],
+        gains.reshape(norm_gains.shape[0], -1),
+        biases.reshape(bias_rows.shape[0], -1),
+        rows[:, nb + ng :].reshape(-1),
+    )
+
+
+def reduce_layer(d_qkv, d_out, d_up, d_down, d_gains, d_biases, d_up_bias):
+    big = [g.astype(BF) for g in (d_down, d_up, d_out, d_qkv)]
+    if not square():
+        def full(g):
+            part = lax.psum_scatter(g, "rep", scatter_dimension=1, tiled=True).astype(F32)
+            part = lax.psum_scatter(part, "dp", scatter_dimension=0, tiled=True)
+            return lax.all_gather(part.astype(BF), "rep", axis=1, tiled=True).astype(F32)
+
+        down, up, out, qkv = [full(g) for g in big]
+        small = lax.psum(
+            (
+                lax.psum_scatter(d_gains, "dp", scatter_dimension=1, tiled=True),
+                lax.psum_scatter(d_biases, "dp", scatter_dimension=1, tiled=True),
+                lax.psum_scatter(d_up_bias, "dp", scatter_dimension=0, tiled=True),
+            ),
+            "rep",
+        )
+        return (qkv, out, up, down) + small
+    def cut(g):
+        return g.reshape(g.shape[0], 8, -1).transpose(1, 0, 2).reshape(8, -1)
+
+    parts = [cut(d_gains), cut(d_biases), d_up_bias.reshape(8, -1)]
+    small = jnp.concatenate(parts, 1)
+    small = jnp.pad(small, ((0, 0), (0, 48 * 128 - small.shape[1]))).reshape(8 * 48, 128)
+    down, up, out, qkv, own = scatter(big + [small])
+    own = own.reshape(-1)
+    n0, n1, n2 = (p.shape[1] for p in parts)
+    return (
+        qkv, out, up, down,
+        own[:n0].reshape(d_gains.shape[0], -1),
+        own[n0 : n0 + n1].reshape(d_biases.shape[0], -1),
+        own[n0 + n1 : n0 + n1 + n2],
+    )
 
 
 def token_segments(lengths, owners, device, row_count):
@@ -167,15 +506,7 @@
     query_block = min(512, row_count)
     head_pairs = HEADS // 2
     head_scale = HD ** (-0.5)
-    layer_w = (
-        lax.all_gather(qkv_weight, "dp", axis=0, tiled=True),
-        lax.all_gather(out_weight, "dp", axis=0, tiled=True),
-        lax.all_gather(up_weight, "dp", axis=0, tiled=True),
-        lax.all_gather(down_weight, "dp", axis=0, tiled=True),
-        lax.all_gather(norm_gains, "dp", axis=1, tiled=True),
-        lax.all_gather(bias_rows, "dp", axis=1, tiled=True),
-        lax.all_gather(ff_bias, "dp", axis=0, tiled=True),
-    )
+    layer_w = gather_layer(qkv_weight, out_weight, up_weight, down_weight, norm_gains, bias_rows, ff_bias)
     w_qkv, w_out, w_up, w_down, gains_low, biases_low, up_bias_low = layer_w
     gain_rows = gains_low.astype(jnp.float32)
     shift_rows = biases_low.astype(jnp.float32)
@@ -208,15 +539,6 @@
     )
     live_col = live_rows.astype(jnp.float32)[:, None]
     output = (final_norm * live_col).astype(jnp.bfloat16)
-    gathered_again = (
-        lax.all_gather(qkv_weight, "dp", axis=0, tiled=True),
-        lax.all_gather(out_weight, "dp", axis=0, tiled=True),
-        lax.all_gather(up_weight, "dp", axis=0, tiled=True),
-        lax.all_gather(down_weight, "dp", axis=0, tiled=True),
-        lax.all_gather(norm_gains, "dp", axis=1, tiled=True),
-    )
-    w_qkv, w_out, w_up, w_down, gains_again = gathered_again
-    gain_rows = gains_again.astype(jnp.float32)
     grad_out = cotangent.astype(jnp.float32) * live_col
     d_gain_two = jnp.sum(grad_out * unit_two, axis=0)
     d_shift_two = jnp.sum(grad_out, axis=0)
@@ -266,55 +588,7 @@
             d_shift_two,
         ]
     )
-    column_parts = (
-        lax.psum_scatter(d_qkv.astype(jnp.bfloat16), "rep", scatter_dimension=1, tiled=True).astype(
-            jnp.float32
-        ),
-        lax.psum_scatter(d_out.astype(jnp.bfloat16), "rep", scatter_dimension=1, tiled=True).astype(
-            jnp.float32
-        ),
-        lax.psum_scatter(d_up.astype(jnp.bfloat16), "rep", scatter_dimension=1, tiled=True).astype(
-            jnp.float32
-        ),
-        lax.psum_scatter(
-            d_down.astype(jnp.bfloat16), "rep", scatter_dimension=1, tiled=True
-        ).astype(jnp.float32),
-    )
-    owned = (
-        lax.psum_scatter(column_parts[0], "dp", scatter_dimension=0, tiled=True),
-        lax.psum_scatter(column_parts[1], "dp", scatter_dimension=0, tiled=True),
-        lax.psum_scatter(column_parts[2], "dp", scatter_dimension=0, tiled=True),
-        lax.psum_scatter(column_parts[3], "dp", scatter_dimension=0, tiled=True),
-        lax.psum_scatter(d_gains, "dp", scatter_dimension=1, tiled=True),
-        lax.psum_scatter(d_biases, "dp", scatter_dimension=1, tiled=True),
-        lax.psum_scatter(d_up_bias, "dp", scatter_dimension=0, tiled=True),
-    )
-    small_sums = lax.psum((owned[4], owned[5], owned[6]), "rep")
-    full_rows = (
-        lax.all_gather(owned[0].astype(jnp.bfloat16), "rep", axis=1, tiled=True).astype(
-            jnp.float32
-        ),
-        lax.all_gather(owned[1].astype(jnp.bfloat16), "rep", axis=1, tiled=True).astype(
-            jnp.float32
-        ),
-        lax.all_gather(owned[2].astype(jnp.bfloat16), "rep", axis=1, tiled=True).astype(
-            jnp.float32
-        ),
-        lax.all_gather(owned[3].astype(jnp.bfloat16), "rep", axis=1, tiled=True).astype(
-            jnp.float32
-        ),
-    )
-    return (
-        output,
-        grad_tokens,
-        full_rows[0],
-        full_rows[1],
-        full_rows[2],
-        full_rows[3],
-        small_sums[0],
-        small_sums[1],
-        small_sums[2],
-    )
+    return (output, grad_tokens) + reduce_layer(d_qkv, d_out, d_up, d_down, d_gains, d_biases, d_up_bias)
 
 
 def solution(mesh):

time: 1030 us -> 572 us (0.56)
  waiting for transfers between devices: 473 us -> 0 us
  Pallas kernels: 0 us -> 182 us
  blocking collectives: 146 us -> 0 us
  between operations: 15.4 us -> 1.22 us
    reduce_scatter x6 -> x0, waiting for transfers between devices: 225 us -> none  [the longest x1 58.2 us: local(): lax.psum_scatter(column_parts[2], 'dp', scatter_dimension=0, tiled=True)]
    unnamed x18 -> x0, waiting for transfers between devices: 201 us -> none
    pallas_call x0 -> x2, Pallas kernels: none -> 182 us  [the longest x1 105 us: scatter(): pl.pallas_call(functools.partial(scatter_kernel, n), out_shape=[jax.Shape...]
    all_gather x7 -> x0, blocking collectives: 102 us -> none  [the longest x1 28.6 us: local(): lax.all_gather(bias_rows, 'dp', axis=1, tiled=True)]
    all_gather x4 -> x0, waiting for transfers between devices: 48 us -> none  [the longest x1 42 us: local(): lax.all_gather(down_weight, 'dp', axis=0, tiled=True)]
    unnamed x1 -> x0, blocking collectives: 37.5 us -> none
    unnamed x80 -> x70, local copies, waits for them, and re-layouts: 27.7 us -> 18.6 us
  transfers between devices with their start and end apart: 14 -> 0, of which waited for: 11 -> 0; matrix products, arithmetic and copies ran while one was open for 32% -> 0% of each run, Pallas kernels for 0% -> 0%
where the time goes in v1:
time: 572 us; the launch traced here: 564 us
  matrix products  220 us (38%)
  Pallas kernels  182 us (32%)
  local copies, waits for them, and re-layouts  79.8 us (14%)
  other arithmetic  79.8 us (14%)
    pallas_call x1, Pallas kernels, scatter(): pl.pallas_call(functools.partial(scatter_kernel, n), out_shape=[jax.Shape...  105 us
    pallas_call x1, Pallas kernels, gather(): pl.pallas_call(functools.partial(gather_kernel, n), out_shape=[jax.ShapeD...  76.9 us
    dot_general x1, matrix products, local(): jnp.dot(first_low, w_up, preferred_element_type=jnp.float32) + up_bias  38.1 us
    dot_general x12, matrix products, pair_backward(): jnp.einsum('qhd,khd->hqk', grad_part, value_heads, preferred_element_type...  21.2 us
    or x12, other arithmetic, allowed_block(): return (same_segment | self_pair)[None]  18.9 us
    unnamed x70, local copies, waits for them, and re-layouts  18.6 us
    dot_general x1, matrix products, local(): jnp.einsum('td,fd->tf', grad_ffn, w_down, preferred_element_type=jnp.floa...  17.6 us
    dynamic_slice x18, local copies, waits for them, and re-layouts, local(): mixed_pairs, log_total = lax.map(attend, (queries, keys_all, values_all))  17.6 us

profile of v1, /device:TPU:0, one launch (start us, length us, event | category | flops | bytes accessed | tf_op | source)
XLA Modules:
  0.0 564.1 jit_solution(8304132997679614760)
XLA Ops:
  3.5 76.9 %gather.1 = (bf16[4,2,2,3,16,128]{5,4,3,2,1,0:T(8,128)(2,1)}, bf16[4,2,2,3,16,2304]{5,4,3,2,1,0:T(8,128)(2,1)}, bf16[4,2,2,3,16,768]{5,4,3,2,1,0:T(8,128)(2,1)},...) custom-call(bf16[2,3,16,128]{3,2,1,0:T(8,128)(2,1)} %bitcast.294, ...), custom_call_target="tpu_custom_call" | custom-call | tf_op jit(solution)/shard_map/gather/pallas_call | solution.py:149
  82.6 6.9 %fusion.39 = bf16[1024,2304]{0,1:T(8,128)(2,1)S(1)} fusion(bf16[768,2304]{1,0:T(8,128)(2,1)} %bitcast.301, bf16[1024,768]{1,0:T(8,128)(2,1)} %param.15, f32[2304]{0:T(1024)S(1)} %pad_maximum_fusion.1), kind=kOutput, calls=%fused_computation.92 | convolution fusion | flops 3628597248 | bytes 9839616 | tf_op jit(solution)/shard_map/dot_general | solution.py:516
  89.5 2.2 fusion.60
  92.4 3.8 scatter_custom_fusion
  100.1 74.5 %while.26 = (s32[]{:T(128)}, bf16[6,1024,128]{1,2,0:T(8,128)(2,1)}, f32[6,2,1024]{2,1,0:T(2,128)}, bf16[6,1024,128]{1,2,0:T(8,128)(2,1)}, s32[1024]{0:T(1024)S(1...) while((s32[]{:T(128)}, bf16[6,1024,128]{1,2,0:T(8,128)(2,1)}, ...), condition=%wide.region_10.11_spmd, body=%wide.region_5.10_spmd.sunk | while | flops 567804416 | bytes 33137796 | solution.py:526
  100.1 1.6 fusion.165
  108.8 1.5 fusion.171
  110.3 1.5 fusion.168
  112.5 1.6 fusion.165
  121.2 1.4 fusion.171
  122.7 1.5 fusion.168
  124.9 1.6 fusion.165
  133.6 1.4 fusion.171
  135.1 1.5 fusion.168
  137.3 1.6 fusion.165
  146.1 1.5 fusion.171
  147.5 1.5 fusion.168
  149.7 1.6 fusion.165
  158.5 1.5 fusion.171
  159.9 1.5 fusion.168
  162.2 1.6 fusion.165
  170.9 1.5 fusion.171
  172.4 1.5 fusion.168
  175.7 2.6 copy.27
  178.3 3.8 fusion.62
  182.7 38.1 %multiply_convert_fusion.2 = (bf16[1024,3072]{1,0:T(8,128)(2,1)}, f32[1024,3072]{1,0:T(8,128)}, f32[1024,3072]{1,0:T(8,128)}) fusion(f32[3072]{0:T(1024)S(1)} %reshape.632, bf16[768,3072]{1,0:T(8,128)(2,1)} %bitcast.297, f32[1024,768]{0,1:T(8,128)S(1)} %get-tuple-element.256, f32[768]{0:T(1024)S(1)} %add.159, f32[768]{0:T(1024)S(1)} %mul.185, ...), kind=kOutput, calls=%fused_computation.73 | convolution fusion | flops 5043388416 | bytes 39348224 | tf_op jit(solution)/shard_map/dot_general | solution.py:533
  220.9 9.6 %fusion.63 = (f32[1024]{0:T(1024)S(1)}, f32[1024,768]{0,1:T(8,128)S(1)}) fusion(f32[768]{0:T(1024)S(1)} %add.164, bf16[1024,3072]{1,0:T(8,128)(2,1)} %get-tuple-element.212, bf16[3072,768]{1,0:T(8,128)(2,1)} %bitcast.299, f32[768]{0:T(1024)S(1)} %add.159, f32[768]{0:T(1024)S(1)} %mul.185, f32[1024]{0:T(1024)S(1)} %add_rsqrt_fusion.1, ...), kind=kOutput, calls=%fused_computation.167 | convolution fusion | flops 4837342208 | bytes 17323008 | tf_op jit(solution)/shard_map/dot_general | solution.py:536
  231.0 2.6 copy.29
  233.6 3.4 multiply_reduce_fusion.2
  237.1 4.6 convert_reduce_fusion.2
  241.6 17.6 %convert_reduce_fusion = (f32[3072]{0:T(1024)S(1)}, bf16[1024,3072]{1,0:T(8,128)(2,1)}) fusion(f32[1024,3072]{1,0:T(8,128)} %get-tuple-element.213, bf16[1024,768]{0,1:T(8,128)(2,1)S(1)} %get-tuple-element.209, bf16[3072,768]{1,0:T(8,128)(2,1)} %bitcast.300, f32[1024,3072]{1,0:T(8,128)} %get-tuple-element.257, f32[3072]{0:T(1024)S(1)} %reshape.632), kind=kOutput, calls=%fused_computation.71 | convolution fusion | flops 4885312512 | bytes 37773312 | tf_op jit(solution)/shard_map/td,fd->tf/dot_general | solution.py:549
  259.3 10.9 %multiply_reduce_fusion.3 = (f32[768]{0:T(1024)S(1)}, f32[1024]{0:T(1024)S(1)}, f32[1024]{0:T(1024)S(1)}, f32[768]{0:T(1024)S(1)}, f32[1024,768]{0,1:T(8,128)S(1)}) fusion(f32[1024,768]{0,1:T(8,128)} %copy-done.1, f32[1024]{0:T(1024)S(1)} %add_rsqrt_fusion.1, f32[1024]{0:T(1024)S(1)} %broadcast_multiply_fusion.5, f32[768]{0:T(1024)S(1)} %mul.185, ...), kind=kOutput, calls=%fused_computation.97 | convolution fusion | flops 4846776320 | bytes 22069248 | tf_op jit(solution)/shard_map/tf,df->td/dot_general | solution.py:553
  271.5 2.6 convolution_convert_fusion.3
  275.6 1.4 broadcast.319.clone.2
  277.0 124.1 %while.27 = (s32[]{:T(128)}, bf16[6,1024,128]{1,2,0:T(8,128)(2,1)S(1)}, bf16[6,1024,128]{1,2,0:T(8,128)(2,1)}, bf16[6,1024,128]{1,2,0:T(8,128)(2,1)}, bf16[6,102...) while((s32[]{:T(128)}, ...), condition=%wide.region_22.23_spmd, body=%wide.region_19.22_spmd.sunk | while | flops 1380317696 | bytes 76383400 | solution.py:569
  280.2 1.6 fusion.198
  284.4 1.8 multiply_reduce_fusion.12
  288.7 1.8 multiply_reduce_fusion.11
  300.8 1.6 fusion.198
  305.0 1.8 multiply_reduce_fusion.12
  309.4 1.8 multiply_reduce_fusion.11
  321.4 1.6 fusion.198
  325.7 1.8 multiply_reduce_fusion.12
  330.0 1.8 multiply_reduce_fusion.11
  342.0 1.6 fusion.198
  346.3 1.8 multiply_reduce_fusion.12
  350.6 1.8 multiply_reduce_fusion.11
  362.6 1.6 fusion.198
  366.9 1.8 multiply_reduce_fusion.12
  371.2 1.8 multiply_reduce_fusion.11
  383.2 1.6 fusion.198
  387.5 1.8 multiply_reduce_fusion.12
  391.8 1.8 multiply_reduce_fusion.11
  401.1 2.4 convert_reduce_fusion.1
  405.3 8.1 %convolution_convert_fusion.2 = bf16[2304,768]{0,1:T(8,128)(2,1)} fusion(bf16[1024,768]{1,0:T(8,128)(2,1)} %param.15, bf16[1024,768]{0,1:T(8,128)(2,1)} %bitcast.272, bf16[1024,768]{0,1:T(8,128)(2,1)} %bitcast.269, bf16[1024,768]{0,1:T(8,128)(2,1)S(1)} %bitcast.266), kind=kOutput, calls=%fused_computation.91 | convolution fusion | flops 3639803904 | bytes 9830400 | tf_op jit(solution)/shard_map/td,te->de/dot_general | solution.py:576
  413.4 4.0 convolution_convert_fusion.4
  417.5 9.9 %convolution_convert_fusion = bf16[768,3072]{1,0:T(8,128)(2,1)} fusion(bf16[1024,3072]{1,0:T(8,128)(2,1)} %get-tuple-element.262, f32[1024,768]{0,1:T(8,128)S(1)} %copy-done.3, f32[768]{0:T(1024)S(1)} %copy-done.25, f32[768]{0:T(1024)S(1)} %mul.185, f32[1024]{0:T(1024)S(1)} %add_rsqrt_fusion.1, f32[1024]{0:T(1024)S(1)} %broadcast_multiply_fusion.5), kind=kOutput, calls=%fused_computation.89 | convolution fusion | flops 4838129664 | bytes 14170112 | tf_op jit(solution)/shard_map/td,tf->df/dot_general | solution.py:552
  427.4 7.0 %convolution_convert_fusion.1 = bf16[3072,768]{1,0:T(8,128)(2,1)} fusion(bf16[1024,3072]{1,0:T(8,128)(2,1)S(1)} %bitcast.306, bf16[1024,768]{0,1:T(8,128)(2,1)S(1)} %copy-done.11), kind=kOutput, calls=%fused_computation.90 | convolution fusion | flops 4834197504 | bytes 12582912 | tf_op jit(solution)/shard_map/tf,td->fd/dot_general | solution.py:548
  434.4 105.4 %scatter.2 = (f32[2,3,64,768]{3,2,1,0:T(8,128)}, f32[2,3,16,3072]{3,2,1,0:T(8,128)}, f32[2,3,16,768]{3,2,1,0:T(8,128)}, f32[2,3,16,2304]{3,2,1,0:T(8,128)}, f32[2,3,8,128]{3,2,1,0:T(8,128)}) custom-call(bf16[4,2,2,3,64,768]{5,4,3,2,1,0:T(8,128)(2,1)} %bitcast.275, bf16[4,2,2,3,16,3072]{5,4,3,2,1,0:T(8,128)(2,1)} %bitcast.274, ...), custom_call_target="tpu_custom_call" | custom-call | tf_op jit(solution)/shard_map/scatter/pallas_call | solution.py:274
  543.1 9.4 %convolution_add_fusion.2 = f32[1024,768]{0,1:T(8,128)} fusion(f32[1024,768]{0,1:T(8,128)} %copy-done.6, bf16[768,2304]{1,0:T(8,128)(2,1)} %bitcast.302, bf16[1024,768]{0,1:T(8,128)(2,1)} %bitcast.273, bf16[1024,768]{0,1:T(8,128)(2,1)} %bitcast.270, bf16[1024,768]{0,1:T(8,128)(2,1)S(1)} %bitcast.267), kind=kOutput, calls=%fused_computation.117 | convolution fusion | flops 3638820864 | bytes 14548992 | tf_op jit(solution)/shard_map/te,de->td/dot_general | solution.py:577
  552.4 3.7 copy.33
  556.1 1.6 copy.32
  557.7 2.1 copy.68
  560.5 2.4 copy.70
  (336 shorter events, 161.0 us)
Async XLA Ops:
  89.5 2.3 copy-start.23
  89.5 2.3 copy-start.26
  174.6 1.1 copy-start.4
  174.6 7.5 %copy-start.8 = (s32[1024]{0:T(1024)}, s32[1024]{0:T(1024)S(1)}, u32[]{:S(2)}) copy-start(s32[1024]{0:T(1024)S(1)} %get-tuple-element.545) | copy-start | bytes 12292
  174.6 7.5 %copy-start.13 = (pred[1024]{0:T(1024)(128)(4,1)}, pred[1024]{0:T(1024)(128)(4,1)S(1)}, u32[]{:S(2)}) copy-start(pred[1024]{0:T(1024)(128)(4,1)S(1)} %get-tuple-element.546) | copy-start | bytes 3076
  182.1 38.7 %copy-start.1 = (f32[1024,768]{0,1:T(8,128)}, f32[1024,768]{0,1:T(8,128)S(1)}, u32[]{:S(2)}) copy-start(f32[1024,768]{0,1:T(8,128)S(1)} %get-tuple-element.256) | copy-start | bytes 9437188
  182.7 38.2 %copy-start.24 = (f32[768]{0:T(1024)}, f32[768]{0:T(1024)S(1)}, u32[]{:S(2)}) copy-start(f32[768]{0:T(1024)S(1)} %add.159) | copy-start | bytes 9220
  182.7 38.1 %copy-start.22 = (f32[8,96]{1,0:T(8,128)S(1)}, f32[8,96]{1,0:T(8,128)}, u32[]{:S(2)}) copy-start(f32[8,96]{1,0:T(8,128)} %get-tuple-element.163) | copy-start | bytes 9220
  220.9 10.1 %copy-start.21 = (f32[8,96]{1,0:T(8,128)S(1)}, f32[8,96]{1,0:T(8,128)}, u32[]{:S(2)}) copy-start(f32[8,96]{1,0:T(8,128)} %get-tuple-element.264) | copy-start | bytes 9220
  230.5 3.1 copy-start.16
  230.9 6.1 %copy-start.20 = (f32[8,96]{1,0:T(8,128)S(1)}, f32[8,96]{1,0:T(8,128)}, u32[]{:S(2)}) copy-start(f32[8,96]{1,0:T(8,128)} %get-tuple-element.162) | copy-start | bytes 9220
  241.6 17.6 %copy-start.10 = (bf16[1024,768]{0,1:T(8,128)(2,1)}, bf16[1024,768]{0,1:T(8,128)(2,1)S(1)}, u32[]{:S(2)}) copy-start(bf16[1024,768]{0,1:T(8,128)(2,1)S(1)} %get-tuple-element.209) | copy-start | bytes 4718596
  241.6 17.6 %copy-start = (bf16[1024,768]{0,1:T(8,128)(2,1)S(1)}, bf16[1024,768]{0,1:T(8,128)(2,1)}, u32[]{:S(2)}) copy-start(bf16[1024,768]{0,1:T(8,128)(2,1)} %copy.29) | copy-start | bytes 4718596
  259.3 11.0 %copy-start.2 = (f32[1024,768]{0,1:T(8,128)S(1)}, f32[1024,768]{0,1:T(8,128)}, u32[]{:S(2)}) copy-start(f32[1024,768]{0,1:T(8,128)} %copy-done.1) | copy-start | bytes 9437188
  270.3 1.3 copy-start.27
  271.4 2.7 copy-start.6
  274.1 2.9 copy-start.9
  274.1 2.9 copy-start.14
  401.1 2.8 copy-start.19
  401.1 2.9 copy-start.18
  401.1 3.2 copy-start.17
  405.3 8.2 %copy-start.7 = (f32[1024,768]{0,1:T(8,128)S(1)}, f32[1024,768]{0,1:T(8,128)}, u32[]{:S(2)}) copy-start(f32[1024,768]{0,1:T(8,128)} %copy-done.6) | copy-start | bytes 9437188
  413.4 4.0 copy-start.3
  413.4 4.0 copy-start.25
  413.4 14.0 %slice-start = ((s8[6291456]{0:T(1024)(128)(4,1)}), s8[4194304]{0:T(1024)(128)(4,1)S(1)}, s32[]{:S(2)}) async-start(s8[6291456]{0:T(1024)(128)(4,1)} %bitcast.305), calls=%async_computation | async-start | bytes 8388608
  417.5 9.9 %copy-start.11 = (bf16[1024,768]{0,1:T(8,128)(2,1)S(1)}, bf16[1024,768]{0,1:T(8,128)(2,1)}, u32[]{:S(2)}) copy-start(bf16[1024,768]{0,1:T(8,128)(2,1)} %copy-done.10) | copy-start | bytes 4718596
  417.5 9.9 %slice-start.1 = ((s8[6291456]{0:T(1024)(128)(4,1)}), s8[2097152]{0:T(1024)(128)(4,1)S(1)}, s32[]{:S(2)}) async-start(s8[6291456]{0:T(1024)(128)(4,1)} %bitcast.305), calls=%async_computation.1 | async-start | bytes 4194304
  552.4 3.7 copy-start.5
  552.4 7.4 %copy-start.15 = (f32[2,3,16,768]{3,2,1,0:T(8,128)S(1)}, f32[2,3,16,768]{3,2,1,0:T(8,128)}, u32[]{:S(2)}) copy-start(f32[2,3,16,768]{3,2,1,0:T(8,128)} %get-tuple-element.132) | copy-start | bytes 884740
  556.1 6.8 %copy-start.12 = (f32[2,3,64,768]{3,2,1,0:T(8,128)S(1)}, f32[2,3,64,768]{3,2,1,0:T(8,128)}, u32[]{:S(2)}) copy-start(f32[2,3,64,768]{3,2,1,0:T(8,128)} %get-tuple-element.134) | copy-start | bytes 3538948

commit v2 on v1

--- a/solution.py
+++ b/solution.py
@@ -36,6 +36,129 @@
 
 def params(**kw):
     return pltpu.CompilerParams(vmem_limit_bytes=VMEM_LIMIT, **kw)
+
+
+def prep_kernel(per, me_ref, own_ref, len_ref, tok_ref, cot_ref, tok_out, cot_out, tab_ref, wide):
+    total = own_ref.shape[0]
+    rows = tok_ref.shape[0]
+    me = me_ref[0]
+
+    def zero(i, c):
+        tab_ref[0, i] = 0
+        return c
+
+    lax.fori_loop(0, 128, zero, 0)
+
+    def scan(p, c):
+        count, start = c
+        hit = own_ref[p] == me
+        size = len_ref[p]
+        tab_ref[0, count] = start
+        tab_ref[0, 16 + count] = size
+        return (count + hit.astype(jnp.int32), start + jnp.where(hit, size, 0))
+
+    lax.fori_loop(0, total, scan, (jnp.int32(0), jnp.int32(0)), unroll=8)
+
+    def find(j, c):
+        return jnp.where(tab_ref[0, 16 + j] > SHORT, j, c)
+
+    big = lax.fori_loop(0, per, find, jnp.int32(0))
+
+    def place(j, slot):
+        is_big = j == big
+        tab_ref[0, 32 + j] = jnp.where(is_big, 0, LONG + SHORT * slot)
+        tab_ref[0, 48 + j] = jnp.where(is_big, LONG // SHORT, 1)
+        at = jnp.where(is_big, 0, slot + 1)
+        tab_ref[0, 64 + at] = tab_ref[0, 16 + j]
+        return slot + jnp.where(is_big, 0, 1)
+
+    lax.fori_loop(0, per, place, jnp.int32(0))
+
+    for src, dst in ((tok_ref, tok_out), (cot_ref, cot_out)):
+        wide[pl.ds(0, rows), :] = src[...].astype(F32)
+        wide[pl.ds(rows, LONG + 8), :] = jnp.zeros((LONG + 8, src.shape[1]), F32)
+
+        def passage(j, c):
+            start = tab_ref[0, j]
+            size = tab_ref[0, 16 + j]
+            to = tab_ref[0, 32 + j]
+
+            def chunk(k, c2):
+                first = start + k * SHORT
+                shift = first % 8
+                piece = wide[pl.ds(pl.multiple_of(first - shift, 8), SHORT + 8), :]
+                piece = pltpu.roll(piece, (SHORT + 8 - shift) % (SHORT + 8), 0)[:SHORT]
+                row = lax.broadcasted_iota(jnp.int32, piece.shape, 0) + k * SHORT
+                dst[pl.ds(pl.multiple_of(to + k * SHORT, SHORT), SHORT), :] = jnp.where(
+                    row < size, piece, 0.0
+                ).astype(BF)
+                return c2
+
+            return lax.fori_loop(0, tab_ref[0, 48 + j], chunk, c)
+
+        lax.fori_loop(0, per, passage, 0)
+
+
+def prep(me, owners, lengths, tokens, cotangent, per):
+    rows, width = tokens.shape
+    return pl.pallas_call(
+        functools.partial(prep_kernel, per),
+        out_shape=(
+            jax.ShapeDtypeStruct((rows, width), BF),
+            jax.ShapeDtypeStruct((rows, width), BF),
+            jax.ShapeDtypeStruct((1, 128), jnp.int32),
+        ),
+        in_specs=[sm(), sm(), sm(), vm(), vm()],
+        out_specs=(vm(), vm(), sm()),
+        scratch_shapes=[pltpu.VMEM((rows + LONG + 8, width), F32)],
+        compiler_params=params(),
+        name="prep",
+    )(me, owners, lengths, tokens, cotangent)
+
+
+def unperm_rows(per, tab_ref, src_ref, wide, mask):
+    rows = src_ref.shape[0]
+    wide[...] = jnp.zeros_like(wide)
+
+    def passage(j, c):
+        start = tab_ref[0, j]
+        size = tab_ref[0, 16 + j]
+        frm = tab_ref[0, 32 + j]
+
+        def chunk(k, c2):
+            piece = src_ref[pl.ds(pl.multiple_of(frm + k * SHORT, SHORT), SHORT), :].astype(F32)
+            row = lax.broadcasted_iota(jnp.int32, piece.shape, 0) + k * SHORT
+            first = start + k * SHORT
+            shift = first % 8
+            at = pl.ds(pl.multiple_of(first - shift, 8), SHORT + 8)
+            piece = jnp.where(row < size, piece, 0.0)
+            piece = jnp.concatenate([piece, jnp.zeros((8, piece.shape[1]), F32)], 0)
+            piece = pltpu.roll(piece, shift, 0)
+            row = lax.broadcasted_iota(jnp.int32, piece.shape, 0)
+            wide[at, :] = jnp.where(row >= shift, piece, wide[at, :])
+            return c2
+
+        return lax.fori_loop(0, tab_ref[0, 48 + j], chunk, c)
+
+    lax.fori_loop(0, per, passage, 0)
+
+
+def unperm_kernel(per, tab_ref, src_ref, out_ref, wide):
+    unperm_rows(per, tab_ref, src_ref, wide, True)
+    out_ref[...] = wide[pl.ds(0, src_ref.shape[0]), :].astype(out_ref.dtype)
+
+
+def unperm(tab, src, per):
+    rows, width = src.shape
+    return pl.pallas_call(
+        functools.partial(unperm_kernel, per),
+        out_shape=jax.ShapeDtypeStruct((rows, width), src.dtype),
+        in_specs=[sm(), vm()],
+        out_specs=vm(),
+        scratch_shapes=[pltpu.VMEM((rows + LONG + 8, width), F32)],
+        compiler_params=params(),
+        name="unperm",
+    )(tab, src)
 
 
 def place_of():
@@ -282,6 +405,121 @@
         name="scatter",
     )(*views)
     return [o.reshape(g.shape[0] // 8, g.shape[1]) for o, g in zip(outs, grads)]
+
+
+def head_lanes(block, head):
+    lane = lax.broadcasted_iota(jnp.int32, (1, block.shape[1]), 1)
+    keep = jnp.where(lane >= HD, float(head), 1.0 - head)
+    return block * keep.astype(BF)
+
+
+def softmax_keys(scores, valid):
+    scores = jnp.where(valid, scores, masked_score)
+    weights = jnp.exp(scores - jnp.max(scores, axis=0, keepdims=True))
+    return weights * (1.0 / jnp.sum(weights, axis=0, keepdims=True))
+
+
+def short_valid(tab_ref, pair, size):
+    key = lax.broadcasted_iota(jnp.int32, (size, size), 0)
+    query = lax.broadcasted_iota(jnp.int32, (size, size), 1)
+    low, high = tab_ref[0, 65 + 2 * pair], tab_ref[0, 66 + 2 * pair]
+    bound = jnp.where(key >= SHORT, SHORT + high, low)
+    return (key < bound) & (key // SHORT == query // SHORT)
+
+
+def attend_kernel(scale, tab_ref, q_ref, k_ref, v_ref, out_ref, long_ref, short_ref):
+    two = 2 * SHORT
+    key = lax.broadcasted_iota(jnp.int32, (LONG, LONG), 0)
+    valid = key < tab_ref[0, 64]
+    shorts = (q_ref.shape[0] - LONG) // two
+    keeps = [short_valid(tab_ref, b, two) for b in range(shorts)]
+    total = None
+    tails = [None] * shorts
+    for h in range(2):
+        scores = dot(head_lanes(k_ref[0:LONG], h), q_ref[0:LONG], NT) * scale
+        probs = softmax_keys(scores, valid).astype(BF)
+        long_ref[h] = probs
+        part = dot(probs, head_lanes(v_ref[0:LONG], h), TN)
+        total = part if total is None else total + part
+        for b in range(shorts):
+            rows = slice(LONG + b * two, LONG + (b + 1) * two)
+            scores = dot(head_lanes(k_ref[rows], h), q_ref[rows], NT) * scale
+            probs = softmax_keys(scores, keeps[b]).astype(BF)
+            short_ref[h, b * two : (b + 1) * two] = probs
+            part = dot(probs, head_lanes(v_ref[rows], h), TN)
+            tails[b] = part if tails[b] is None else tails[b] + part
+    out_ref[0:LONG] = total.astype(BF)
+    for b in range(shorts):
+        out_ref[LONG + b * two : LONG + (b + 1) * two] = tails[b].astype(BF)
+
+
+def attend(tab, projected):
+    rows, wide = projected.shape
+    width = wide // 3
+    pairs = width // (2 * HD)
+    column = lambda off: pl.BlockSpec((rows, 2 * HD), lambda i, off=off: (0, off + i))
+    return pl.pallas_call(
+        functools.partial(attend_kernel, HD ** (-0.5)),
+        grid=(pairs,),
+        out_shape=(
+            jax.ShapeDtypeStruct((rows, width), BF),
+            jax.ShapeDtypeStruct((2 * pairs, LONG, LONG), BF),
+            jax.ShapeDtypeStruct((2 * pairs, rows - LONG, 2 * SHORT), BF),
+        ),
+        in_specs=[sm(), column(0), column(pairs), column(2 * pairs)],
+        out_specs=(
+            column(0),
+            pl.BlockSpec((2, LONG, LONG), lambda i: (i, 0, 0)),
+            pl.BlockSpec((2, rows - LONG, 2 * SHORT), lambda i: (i, 0, 0)),
+        ),
+        compiler_params=params(),
+        name="attend",
+    )(tab, projected, projected, projected)
+
+
+def attend_back_kernel(scale, q_ref, k_ref, v_ref, g_ref, long_ref, short_ref, out_ref):
+    two = 2 * SHORT
+    shorts = (q_ref.shape[0] - LONG) // two
+    spans = [(slice(0, LONG), None)]
+    spans += [(slice(LONG + b * two, LONG + (b + 1) * two), b) for b in range(shorts)]
+    for rows, b in spans:
+        sums = None
+        for h in range(2):
+            probs = long_ref[h] if b is None else short_ref[h, b * two : (b + 1) * two]
+            grad = head_lanes(g_ref[rows], h)
+            wide = probs.astype(F32)
+            grad_probs = dot(v_ref[rows], grad, NT)
+            mean = jnp.sum(grad_probs * wide, axis=0, keepdims=True)
+            grad_scores = (wide * (grad_probs - mean)).astype(BF)
+            parts = (
+                dot(grad_scores, head_lanes(k_ref[rows], h), TN),
+                dot(grad_scores, head_lanes(q_ref[rows], h)),
+                dot(probs, grad),
+            )
+            sums = parts if sums is None else tuple(a + p for a, p in zip(sums, parts))
+        out_ref[0, rows] = (sums[0] * scale).astype(BF)
+        out_ref[1, rows] = (sums[1] * scale).astype(BF)
+        out_ref[2, rows] = sums[2].astype(BF)
+
+
+def attend_back(projected, grad_mixed, long_probs, short_probs):
+    rows, wide = projected.shape
+    width = wide // 3
+    pairs = width // (2 * HD)
+    column = lambda off: pl.BlockSpec((rows, 2 * HD), lambda i, off=off: (0, off + i))
+    return pl.pallas_call(
+        functools.partial(attend_back_kernel, HD ** (-0.5)),
+        grid=(pairs,),
+        out_shape=jax.ShapeDtypeStruct((3, rows, width), BF),
+        in_specs=[
+            column(0), column(pairs), column(2 * pairs), column(0),
+            pl.BlockSpec((2, LONG, LONG), lambda i: (i, 0, 0)),
+            pl.BlockSpec((2, rows - LONG, 2 * SHORT), lambda i: (i, 0, 0)),
+        ],
+        out_specs=pl.BlockSpec((3, rows, 2 * HD), lambda i: (0, 0, i)),
+        compiler_params=params(),
+        name="attend_back",
+    )(projected, projected, projected, grad_mixed, long_probs, short_probs)
 
 
 def square():
@@ -350,19 +588,6 @@
     )
 
 
-def token_segments(lengths, owners, device, row_count):
-    own_mask = owners == device
-    own_sizes = jnp.where(own_mask, lengths, 0)
-    end_points = jnp.cumsum(own_sizes)
-    start_points = jnp.where(own_mask, end_points - own_sizes, row_count)
-    start_marks = (
-        jnp.zeros((row_count + 1,), jnp.int32).at[start_points].add(jnp.ones_like(start_points))
-    )
-    segment = jnp.cumsum(start_marks[:row_count])
-    live_rows = jnp.arange(row_count, dtype=jnp.int32) < end_points[-1]
-    return (segment, live_rows)
-
-
 def normalize_keep(residual, gain_row, shift_row):
     center = residual - jnp.mean(residual, axis=-1, keepdims=True)
     scale_inv = lax.rsqrt(jnp.mean(center * center, axis=-1, keepdims=True) + norm_eps)
@@ -376,114 +601,6 @@
         scaled
         - jnp.mean(scaled, axis=-1, keepdims=True)
         - unit_rows * jnp.mean(scaled * unit_rows, axis=-1, keepdims=True)
-    )
-
-
-def allowed_block(segment, live_rows, row_start, query_block):
-    row_count = segment.shape[0]
-    stop_row = row_start + query_block
-    same_segment = (
-        (segment[row_start:stop_row, None] == segment[None, :])
-        & live_rows[row_start:stop_row, None]
-        & live_rows[None, :]
-    )
-    self_pair = jnp.arange(query_block)[:, None] + row_start == jnp.arange(row_count)[None, :]
-    return (same_segment | self_pair)[None]
-
-
-def split_pairs(matrix, head_pairs):
-    row_count = matrix.shape[0]
-    return matrix.reshape(row_count, head_pairs, -1).transpose(1, 0, 2)
-
-
-def join_pairs(stacked):
-    row_count = stacked.shape[1]
-    return stacked.transpose(1, 0, 2).reshape(row_count, -1)
-
-
-def pair_forward(pieces, segment, live_rows, query_block, head_scale):
-    queries, keys_pair, values_pair = pieces
-    row_count = queries.shape[0]
-    head_width = queries.shape[1] // 2
-    query_heads = queries.reshape(row_count, 2, head_width)
-    key_heads = keys_pair.reshape(row_count, 2, head_width)
-    value_heads = values_pair.reshape(row_count, 2, head_width)
-    out_blocks = []
-    total_blocks = []
-    for row_start in range(0, row_count, query_block):
-        allowed = allowed_block(segment, live_rows, row_start, query_block)
-        scores = (
-            jnp.einsum(
-                "qhd,khd->hqk",
-                query_heads[row_start : row_start + query_block],
-                key_heads,
-                preferred_element_type=jnp.float32,
-            )
-            * head_scale
-        )
-        scores = jnp.where(allowed, scores, masked_score)
-        row_max = jnp.max(scores, axis=-1, keepdims=True)
-        exp_scores = jnp.exp(scores - row_max)
-        row_sum = jnp.sum(exp_scores, axis=-1, keepdims=True)
-        attn_probs = (exp_scores / row_sum).astype(jnp.bfloat16)
-        attended = jnp.einsum(
-            "hqk,khd->qhd", attn_probs, value_heads, preferred_element_type=jnp.float32
-        )
-        out_blocks.append(attended.reshape(query_block, 2 * head_width))
-        total_blocks.append((row_max + jnp.log(row_sum))[:, :, 0])
-    return (jnp.concatenate(out_blocks, 0), jnp.concatenate(total_blocks, 1))
-
-
-def pair_backward(pieces, segment, live_rows, query_block, head_scale):
-    queries, keys_pair, values_pair, grad_pair, log_total = pieces
-    row_count = queries.shape[0]
-    head_width = queries.shape[1] // 2
-    query_heads = queries.reshape(row_count, 2, head_width)
-    key_heads = keys_pair.reshape(row_count, 2, head_width)
-    value_heads = values_pair.reshape(row_count, 2, head_width)
-    grad_heads = grad_pair.reshape(row_count, 2, head_width)
-    grad_key = jnp.zeros((row_count, 2, head_width), jnp.float32)
-    grad_value = jnp.zeros((row_count, 2, head_width), jnp.float32)
-    query_grads = []
-    for row_start in range(0, row_count, query_block):
-        stop_row = row_start + query_block
-        query_part = query_heads[row_start:stop_row]
-        grad_part = grad_heads[row_start:stop_row]
-        allowed = allowed_block(segment, live_rows, row_start, query_block)
-        scores = (
-            jnp.einsum("qhd,khd->hqk", query_part, key_heads, preferred_element_type=jnp.float32)
-            * head_scale
-        )
-        scores = jnp.where(allowed, scores, masked_score)
-        attn_probs = jnp.exp(scores - log_total[:, row_start:stop_row, None])
-        grad_probs = jnp.einsum(
-            "qhd,khd->hqk", grad_part, value_heads, preferred_element_type=jnp.float32
-        )
-        grad_scores = (
-            attn_probs * (grad_probs - jnp.sum(grad_probs * attn_probs, axis=-1, keepdims=True))
-        ).astype(jnp.bfloat16)
-        query_grad = (
-            jnp.einsum("hqk,khd->qhd", grad_scores, key_heads, preferred_element_type=jnp.float32)
-            * head_scale
-        )
-        query_grads.append(query_grad.reshape(query_block, 2 * head_width))
-        grad_key = (
-            grad_key
-            + jnp.einsum(
-                "hqk,qhd->khd", grad_scores, query_part, preferred_element_type=jnp.float32
-            )
-            * head_scale
-        )
-        grad_value = grad_value + jnp.einsum(
-            "hqk,qhd->khd",
-            attn_probs.astype(jnp.bfloat16),
-            grad_part,
-            preferred_element_type=jnp.float32,
-        )
-    return (
-        jnp.concatenate(query_grads, 0),
-        grad_key.reshape(row_count, 2 * head_width),
-        grad_value.reshape(row_count, 2 * head_width),
     )
 
 
@@ -502,10 +619,11 @@
 ):
     row_count, model_width = tokens.shape
     device = lax.axis_index("dp") * lax.axis_size("rep") + lax.axis_index("rep")
-    segment, live_rows = token_segments(lengths, owners, device, row_count)
-    query_block = min(512, row_count)
-    head_pairs = HEADS // 2
-    head_scale = HD ** (-0.5)
+    devices = lax.axis_size("dp") * lax.axis_size("rep")
+    per = lengths.shape[0] // devices
+    assert row_count == LONG + SHORT * (per - 1)
+    me = device.astype(jnp.int32).reshape(1)
+    tokens, cotangent, tab = prep(me, owners, lengths, tokens, cotangent, per)
     layer_w = gather_layer(qkv_weight, out_weight, up_weight, down_weight, norm_gains, bias_rows, ff_bias)
     w_qkv, w_out, w_up, w_down, gains_low, biases_low, up_bias_low = layer_w
     gain_rows = gains_low.astype(jnp.float32)
@@ -516,15 +634,7 @@
     projected = (jnp.dot(tokens, w_qkv, preferred_element_type=jnp.float32) + head_bias).astype(
         jnp.bfloat16
     )
-    queries = split_pairs(projected[:, :model_width], head_pairs)
-    keys_all = split_pairs(projected[:, model_width : 2 * model_width], head_pairs)
-    values_all = split_pairs(projected[:, 2 * model_width :], head_pairs)
-
-    def attend(pieces):
-        return pair_forward(pieces, segment, live_rows, query_block, head_scale)
-
-    mixed_pairs, log_total = lax.map(attend, (queries, keys_all, values_all))
-    mixed_rows = join_pairs(mixed_pairs).astype(jnp.bfloat16)
+    mixed_rows, long_probs, short_probs = attend(tab, projected)
     branch = jnp.dot(mixed_rows, w_out, preferred_element_type=jnp.float32) + shift_rows[2]
     first_norm, unit_one, inv_one = normalize_keep(
         tokens.astype(jnp.float32) + branch, gain_rows[0], shift_rows[4]
@@ -537,9 +647,8 @@
     final_norm, unit_two, inv_two = normalize_keep(
         first_norm + ffn_out, gain_rows[1], shift_rows[5]
     )
-    live_col = live_rows.astype(jnp.float32)[:, None]
-    output = (final_norm * live_col).astype(jnp.bfloat16)
-    grad_out = cotangent.astype(jnp.float32) * live_col
+    output = unperm(tab, final_norm.astype(BF), per)
+    grad_out = cotangent.astype(jnp.float32)
     d_gain_two = jnp.sum(grad_out * unit_two, axis=0)
     d_shift_two = jnp.sum(grad_out, axis=0)
     grad_two = normalize_back(grad_out, unit_two, inv_two, gain_rows[1])
@@ -563,20 +672,14 @@
         "te,de->td", grad_branch, w_out, preferred_element_type=jnp.float32
     ).astype(jnp.bfloat16)
 
-    def attend_back(pieces):
-        return pair_backward(pieces, segment, live_rows, query_block, head_scale)
-
-    grad_query, grad_key, grad_value = lax.map(
-        attend_back, (queries, keys_all, values_all, split_pairs(grad_mixed, head_pairs), log_total)
-    )
-    grad_heads = jnp.concatenate(
-        [join_pairs(grad_query), join_pairs(grad_key), join_pairs(grad_value)], 1
-    ).astype(jnp.bfloat16)
+    parts = attend_back(projected, grad_mixed, long_probs, short_probs)
+    grad_heads = jnp.concatenate([parts[0], parts[1], parts[2]], 1)
     d_head_bias = jnp.sum(grad_heads.astype(jnp.float32), axis=0)
     d_qkv = jnp.einsum("td,te->de", tokens, grad_heads, preferred_element_type=jnp.float32)
     grad_tokens = grad_one + jnp.einsum(
         "te,de->td", grad_heads, w_qkv, preferred_element_type=jnp.float32
     )
+    grad_tokens = unperm(tab, grad_tokens, per)
     d_gains = jnp.stack([d_gain_one, d_gain_two])
     d_biases = jnp.stack(
         [

time: 572 us -> 399 us (0.70)
  matrix products: 220 us -> 118 us
  other arithmetic: 79.8 us -> 12.1 us
  local copies, waits for them, and re-layouts: 79.8 us -> 25.1 us
  Pallas kernels: 182 us -> 236 us
    dot_general x84 -> x0, matrix products: 91.8 us -> none  [the longest x12 21.2 us: pair_backward(): jnp.einsum('qhd,khd->hqk', grad_part, value_heads, preferred_element_type...]
    pallas_call x0 -> x5, Pallas kernels: none -> 53.9 us  [the longest x1 18.8 us: attend_back(): pl.pallas_call(functools.partial(attend_back_kernel, HD ** (-0.5)), grid=...]
    slice x45 -> x0, local copies, waits for them, and re-layouts: 20.9 us -> none  [the longest x6 5.97 us: pair_backward(): grad_part = grad_heads[row_start:stop_row]]
    or x12 -> x0, other arithmetic: 18.9 us -> none  [allowed_block(): return (same_segment | self_pair)[None]]
    dynamic_slice x18 -> x0, local copies, waits for them, and re-layouts: 17.6 us -> none  [local(): mixed_pairs, log_total = lax.map(attend, (queries, keys_all, values_all))]
    convert_element_type x12 -> x0, other arithmetic: 15.8 us -> none  [pair_backward(): grad_scores = (attn_probs * (grad_probs - jnp.sum(grad_probs * attn_probs...]
    reduce_sum x12 -> x0, other arithmetic: 13.9 us -> none  [pair_forward(): row_sum = jnp.sum(exp_scores, axis=-1, keepdims=True)]
    dynamic_update_slice x18 -> x0, other arithmetic: 12.7 us -> none  [local(): mixed_pairs, log_total = lax.map(attend, (queries, keys_all, values_all))]
where the time goes in v2:
time: 399 us; the launch traced here: 393 us
  Pallas kernels  236 us (59%)
  matrix products  118 us (30%)
  local copies, waits for them, and re-layouts  25.1 us (6%)
  other arithmetic  12.1 us (3%)
    pallas_call x1, Pallas kernels, scatter(): pl.pallas_call(functools.partial(scatter_kernel, n), out_shape=[jax.Shape...  105 us
    pallas_call x1, Pallas kernels, gather(): pl.pallas_call(functools.partial(gather_kernel, n), out_shape=[jax.ShapeD...  76.9 us
    dot_general x1, matrix products, local(): jnp.dot(first_low, w_up, preferred_element_type=jnp.float32) + up_bias  35.3 us
    dot_general x1, matrix products, local(): jnp.einsum('td,fd->tf', grad_ffn, w_down, preferred_element_type=jnp.floa...  18.9 us
    pallas_call x1, Pallas kernels, attend_back(): pl.pallas_call(functools.partial(attend_back_kernel, HD ** (-0.5)), grid=...  18.8 us
    pallas_call x1, Pallas kernels, attend(): pl.pallas_call(functools.partial(attend_kernel, HD ** (-0.5)), grid=(pair...  15.3 us
    unnamed x50, local copies, waits for them, and re-layouts  13.3 us
    pallas_call x2, Pallas kernels, unperm(): pl.pallas_call(functools.partial(unperm_kernel, per), out_shape=jax.Shape...  10.8 us

profile of v2, /device:TPU:0, one launch (start us, length us, event | category | flops | bytes accessed | tf_op | source)
XLA Modules:
  0.0 392.5 jit_solution(10723328443725749457)
XLA Ops:
  0.6 0.7 reshape.197
  1.4 0.8 reshape.196
  2.2 0.8 concatenate.14
  2.9 0.6 pad.8
  3.5 9.0 %prep.1 = (bf16[1024,768]{1,0:T(8,128)(2,1)}, bf16[1024,768]{1,0:T(8,128)(2,1)}, s32[1,128]{1,0:T(1,128)}) custom-call(s32[1]{0:T(128)} %bitcast.me_ref, s32[288]{0:T(512)} %own_ref.1, s32[288]{0:T(512)} %len_ref.1, bf16[1024,768]{1,0:T(8,128)(2,1)} %tok_ref.1, bf16[1024,768]{1,0:T(8,128)(2,1)} %cot_ref.1), custom_call_target="tpu_custom_call" | custom-call | tf_op jit(solution)/shard_map/prep/pallas_call | solution.py:104
  12.6 76.9 %gather.1 = (bf16[4,2,2,3,16,128]{5,4,3,2,1,0:T(8,128)(2,1)}, bf16[4,2,2,3,16,2304]{5,4,3,2,1,0:T(8,128)(2,1)}, bf16[4,2,2,3,16,768]{5,4,3,2,1,0:T(8,128)(2,1)},...) custom-call(bf16[2,3,16,128]{3,2,1,0:T(8,128)(2,1)} %bitcast.69, ...), custom_call_target="tpu_custom_call" | custom-call | tf_op jit(solution)/shard_map/gather/pallas_call | solution.py:272
  89.5 1.0 reshape_reshape.13
  90.5 0.1 slice_convert_fusion.2
  90.6 0.1 reshape.219
  90.7 0.1 reshape.218
  90.8 0.1 slice_reduce_fusion
  90.9 0.1 add.109
  91.0 0.1 mul.131
  91.5 8.5 %add_convert_fusion.1.q_ref.k_ref.v_ref = bf16[1024,2304]{1,0:T(8,128)(2,1)} fusion(bf16[1024,768]{1,0:T(8,128)(2,1)} %get-tuple-element.26, bf16[768,2304]{1,0:T(8,128)(2,1)} %bitcast.80, f32[2304]{0:T(1024)S(1)} %pad_maximum_fusion.1), kind=kOutput, calls=%fused_computation.19 | convolution fusion | flops 3628597248 | bytes 9839616 | tf_op jit(solution)/shard_map/dot_general | solution.py:634
  100.0 15.3 %attend.1 = (bf16[1024,768]{1,0:T(8,128)(2,1)}, bf16[12,512,512]{2,1,0:T(8,128)(2,1)}, bf16[12,512,128]{2,1,0:T(8,128)(2,1)}) custom-call(s32[1,128]{1,0:T(1,128)} %get-tuple-element.25.tab_ref, bf16[1024,2304]{1,0:T(8,128)(2,1)} %add_convert_fusion.1.q_ref.k_ref.v_ref, bf16[1024,2304]{1,0:T(8,128)(2,1)} %add_convert_fusion.1.q_ref.k_ref.v_ref, ...), custom_call_target="tpu_custom_call" | custom-call | tf_op jit(solution)/shard_map/attend/pallas_call | solution.py:461
  115.3 3.9 %fusion.24 = (f32[1024]{0:T(1024)S(1)}, f32[1024,768]{1,0:T(8,128)S(1)}) fusion(f32[768]{0:T(1024)S(1)} %add.94, bf16[1024,768]{1,0:T(8,128)(2,1)} %get-tuple-element.29, bf16[768,768]{1,0:T(8,128)(2,1)} %bitcast.82, bf16[1024,768]{1,0:T(8,128)(2,1)} %get-tuple-element.26), kind=kOutput, calls=%fused_computation.84 | convolution fusion | flops 1211104256 | bytes 7478272 | tf_op jit(solution)/shard_map/dot_general | solution.py:638
  119.3 0.5 multiply_reduce_fusion.3
  119.9 35.3 %multiply_convert_fusion = (bf16[1024,3072]{1,0:T(8,128)(2,1)S(1)}, f32[1024,3072]{1,0:T(8,128)}, f32[1024,3072]{1,0:T(8,128)}) fusion(f32[3072]{0:T(1024)S(1)} %reshape.217, bf16[768,3072]{1,0:T(8,128)(2,1)S(1)} %bitcast.75, f32[1024,768]{1,0:T(8,128)S(1)} %get-tuple-element.70, f32[768]{0:T(1024)S(1)} %add.99, f32[768]{0:T(1024)S(1)} %mul.131, ...), kind=kOutput, calls=%fused_computation.4 | convolution fusion | flops 5043388416 | bytes 39348224 | tf_op jit(solution)/shard_map/dot_general | solution.py:643
  155.2 5.4 %fusion.25 = (f32[1024]{0:T(1024)S(1)}, f32[1024,768]{1,0:T(8,128)S(1)}) fusion(f32[768]{0:T(1024)S(1)} %add.104, bf16[1024,3072]{1,0:T(8,128)(2,1)S(1)} %get-tuple-element.61, bf16[3072,768]{1,0:T(8,128)(2,1)S(1)} %bitcast.79, f32[768]{0:T(1024)S(1)} %add.99, f32[768]{0:T(1024)S(1)} %mul.131, f32[1024]{0:T(1024)S(1)} %add_rsqrt_fusion.1, ...), kind=kOutput, calls=%fused_computation.85 | convolution fusion | flops 4837342208 | bytes 17323008 | tf_op jit(solution)/shard_map/dot_general | solution.py:646
  160.7 0.5 multiply_reduce_fusion.2
  161.2 0.9 copy-done.2
  162.1 1.7 fusion.12
  163.7 0.1 stack.31
  163.8 4.0 %convert_reduce_fusion.3 = (f32[768]{0:T(1024)S(1)}, f32[1024,768]{1,0:T(8,128)}, bf16[1024,768]{1,0:T(8,128)(2,1)}) fusion(f32[1024]{0:T(1024)S(1)} %broadcast_multiply_fusion.2, f32[1024,768]{1,0:T(8,128)S(1)} %get-tuple-element.73, f32[1024]{0:T(1024)S(1)} %broadcast_multiply_fusion.4, f32[1024]{0:T(1024)S(1)} %broadcast_multiply_fusion.3, ...), kind=kLoop, calls=%fused_computation.34 | loop fusion | flops 11009280 | bytes 9462784 | tf_op jit(solution)/shard_map/reduce_sum | solution.py:656
  167.8 18.9 %convert_reduce_fusion = (f32[3072]{0:T(1024)S(1)}, bf16[1024,3072]{1,0:T(8,128)(2,1)}) fusion(f32[1024,3072]{1,0:T(8,128)} %get-tuple-element.62, bf16[3072,768]{1,0:T(8,128)(2,1)} %bitcast.76, f32[1024,768]{1,0:T(8,128)} %get-tuple-element.58, f32[1024,3072]{1,0:T(8,128)} %get-tuple-element.71, f32[3072]{0:T(1024)S(1)} %reshape.217), kind=kOutput, calls=%fused_computation.2 | convolution fusion | flops 4886098944 | bytes 39346176 | tf_op jit(solution)/shard_map/td,fd->tf/dot_general | solution.py:658
  186.7 9.8 %convolution_convert_fusion.1 = bf16[3072,768]{1,0:T(8,128)(2,1)} fusion(bf16[1024,3072]{1,0:T(8,128)(2,1)} %copy-done.17, f32[1024,768]{1,0:T(8,128)} %get-tuple-element.58), kind=kOutput, calls=%fused_computation.21 | convolution fusion | flops 4834983936 | bytes 14155776 | tf_op jit(solution)/shard_map/tf,td->fd/dot_general | solution.py:657
  196.5 9.9 %multiply_reduce_fusion = (f32[768]{0:T(1024)S(1)}, f32[1024]{0:T(1024)S(1)}, f32[1024]{0:T(1024)S(1)}, f32[768]{0:T(1024)S(1)}, f32[1024,768]{1,0:T(8,128)}) fusion(f32[1024,768]{1,0:T(8,128)S(1)} %copy-done.1, f32[1024]{0:T(1024)S(1)} %add_rsqrt_fusion.1, f32[1024]{0:T(1024)S(1)} %broadcast_multiply_fusion.5, f32[768]{0:T(1024)S(1)} %mul.131, ...), kind=kOutput, calls=%fused_computation.36 | convolution fusion | flops 4839698432 | bytes 20472832 | tf_op jit(solution)/shard_map/tf,df->td/dot_general | solution.py:662
  206.4 0.1 stack.30
  206.5 0.1 reshape.210
  206.6 0.1 stack.36
  206.7 2.9 convert_reduce_fusion.4
  209.5 0.9 copy-done.16
  210.4 7.8 %convolution_convert_fusion = bf16[768,3072]{1,0:T(8,128)(2,1)} fusion(bf16[1024,3072]{1,0:T(8,128)(2,1)S(1)} %copy-done.16, f32[1024,768]{1,0:T(8,128)S(1)} %copy-done.1, f32[768]{0:T(1024)S(1)} %add.99, f32[768]{0:T(1024)S(1)} %mul.131, f32[1024]{0:T(1024)S(1)} %add_rsqrt_fusion.1, f32[1024]{0:T(1024)S(1)} %broadcast_multiply_fusion.5), kind=kOutput, calls=%fused_computation.20 | convolution fusion | flops 4838129664 | bytes 14170112 | tf_op jit(solution)/shard_map/td,tf->df/dot_general | solution.py:661
  218.2 2.5 convolution_convert_fusion.4
  220.7 0.1 stack.35
  220.8 0.1 stack.37
  220.9 0.1 stack.38
  221.0 4.5 %convolution_convert_fusion.3.g_ref = bf16[1024,768]{1,0:T(8,128)(2,1)} fusion(bf16[768,768]{1,0:T(8,128)(2,1)S(1)} %bitcast.83, f32[1024,768]{1,0:T(8,128)} %copy-done.8), kind=kOutput, calls=%fused_computation.51 | convolution fusion | flops 1209532416 | bytes 5898240 | tf_op jit(solution)/shard_map/te,de->td/dot_general | solution.py:671
  225.4 18.8 %attend_back.1 = bf16[3,1024,768]{2,1,0:T(8,128)(2,1)} custom-call(bf16[1024,2304]{1,0:T(8,128)(2,1)} %add_convert_fusion.1.q_ref.k_ref.v_ref, bf16[1024,2304]{1,0:T(8,128)(2,1)} %add_convert_fusion.1.q_ref.k_ref.v_ref, bf16[1024,2304]{1,0:T(8,128)(2,1)} %add_convert_fusion.1.q_ref.k_ref.v_ref, bf16[1024,768]{1,0:T(8,128)(2,1)} %convolution_convert_fusion.3.g_ref, ...), custom_call_target="tpu_custom_call" | custom-call | tf_op jit(solution)/shard_map/attend_back/pallas_call | solution.py:510
  244.2 2.8 slice_bitcast_fusion.2
  247.0 1.1 copy-done.3
  248.2 0.6 copy-done.5
  248.8 0.9 copy-done.11
  249.7 5.5 %convolution_add_fusion.1.src_ref = f32[1024,768]{1,0:T(8,128)} fusion(f32[1024,768]{1,0:T(8,128)S(1)} %copy-done.9, bf16[768,2304]{1,0:T(8,128)(2,1)S(1)} %bitcast.81, bf16[1024,768]{1,0:T(8,128)(2,1)S(1)} %get-tuple-element.64, bf16[1024,768]{1,0:T(8,128)(2,1)S(1)} %get-tuple-element.65, bf16[1024,768]{1,0:T(8,128)(2,1)S(1)} %get-tuple-element.63), kind=kOutput, calls=%fused_computation.50 | convolution fusion | flops 3638820864 | bytes 14548992 | tf_op jit(solution)/shard_map/te,de->td/dot_general | solution.py:679
  255.2 6.1 %unperm.3 = f32[1024,768]{1,0:T(8,128)} custom-call(s32[1,128]{1,0:T(1,128)} %get-tuple-element.25.tab_ref, f32[1024,768]{1,0:T(8,128)} %convolution_add_fusion.1.src_ref), custom_call_target="tpu_custom_call" | custom-call | tf_op jit(solution)/shard_map/unperm/pallas_call | solution.py:153
  261.3 4.6 %unperm.2 = bf16[1024,768]{1,0:T(8,128)(2,1)} custom-call(s32[1,128]{1,0:T(1,128)} %get-tuple-element.25.tab_ref, bf16[1024,768]{1,0:T(8,128)(2,1)} %get-tuple-element.66.src_ref), custom_call_target="tpu_custom_call" | custom-call | tf_op jit(solution)/shard_map/unperm/pallas_call | solution.py:153
  266.0 2.4 convert_reduce_fusion.1
  268.4 0.4 copy-done.6
  268.8 0.5 copy-done.12
  269.3 6.0 %convolution_convert_fusion.2 = bf16[768,2304]{1,0:T(8,128)(2,1)} fusion(bf16[1024,768]{1,0:T(8,128)(2,1)S(1)} %copy-done.12, bf16[1024,768]{1,0:T(8,128)(2,1)S(1)} %copy-done.4, bf16[1024,768]{1,0:T(8,128)(2,1)S(1)} %copy-done.6, bf16[1024,768]{1,0:T(8,128)(2,1)S(1)} %get-tuple-element.63), kind=kOutput, calls=%fused_computation.22 | convolution fusion | flops 3639803904 | bytes 9830400 | tf_op jit(solution)/shard_map/td,te->de/dot_general | solution.py:678
  275.3 0.1 stack.34
  275.4 0.1 stack.33
  275.5 0.1 reshape.211
  275.6 0.1 concatenate.17
  275.7 0.7 copy.23
  276.4 105.1 %scatter.1 = (f32[2,3,64,768]{3,2,1,0:T(8,128)}, f32[2,3,16,3072]{3,2,1,0:T(8,128)}, f32[2,3,16,768]{3,2,1,0:T(8,128)}, f32[2,3,16,2304]{3,2,1,0:T(8,128)}, f32[2,3,8,128]{3,2,1,0:T(8,128)}) custom-call(bf16[4,2,2,3,64,768]{5,4,3,2,1,0:T(8,128)(2,1)} %bitcast.54, bf16[4,2,2,3,16,3072]{5,4,3,2,1,0:T(8,128)(2,1)} %bitcast.55, ...), custom_call_target="tpu_custom_call" | custom-call | tf_op jit(solution)/shard_map/scatter/pallas_call | solution.py:397
  381.5 1.4 slice.125
  382.9 0.8 slice.103
  383.7 0.6 slice.123
  384.3 0.6 slice.124
  384.9 2.1 copy.28
  387.0 1.7 copy.29
  388.7 2.4 copy.30
  391.1 1.0 copy.31
  (63 shorter events, 0.7 us)
Async XLA Ops:
  100.0 19.8 %slice-start = ((s8[4718592]{0:T(1024)(128)(4,1)}), s8[524288]{0:T(1024)(128)(4,1)S(1)}, s32[]{:S(2)}) async-start(s8[4718592]{0:T(1024)(128)(4,1)} %bitcast.73), calls=%async_computation | async-start | bytes 1048576
  115.3 4.5 %slice-start.1 = ((s8[4718592]{0:T(1024)(128)(4,1)}), s8[4194304]{0:T(1024)(128)(4,1)S(1)}, s32[]{:S(2)}) async-start(s8[4718592]{0:T(1024)(128)(4,1)} %bitcast.73), calls=%async_computation.1 | async-start | bytes 8388608
  115.3 39.8 %slice-start.2 = ((s8[4718592]{0:T(1024)(128)(4,1)}), s8[4194304]{0:T(1024)(128)(4,1)S(1)}, s32[]{:S(2)}) async-start(s8[4718592]{0:T(1024)(128)(4,1)} %bitcast.77), calls=%async_computation.2 | async-start | bytes 8388608
  119.3 35.9 %copy-start = (f32[1024,768]{1,0:T(8,128)}, f32[1024,768]{1,0:T(8,128)S(1)}, u32[]{:S(2)}) copy-start(f32[1024,768]{1,0:T(8,128)S(1)} %get-tuple-element.70) | copy-start | bytes 9437188
  119.9 35.3 %slice-start.3 = ((s8[4718592]{0:T(1024)(128)(4,1)}), s8[524288]{0:T(1024)(128)(4,1)S(1)}, s32[]{:S(2)}) async-start(s8[4718592]{0:T(1024)(128)(4,1)} %bitcast.77), calls=%async_computation.3 | async-start | bytes 1048576
  155.2 5.5 %copy-start.17 = (bf16[1024,3072]{1,0:T(8,128)(2,1)}, bf16[1024,3072]{1,0:T(8,128)(2,1)S(1)}, u32[]{:S(2)}) copy-start(bf16[1024,3072]{1,0:T(8,128)(2,1)S(1)} %get-tuple-element.61) | copy-start | bytes 18874372
  160.6 1.4 copy-start.2
  186.7 9.8 %copy-start.1 = (f32[1024,768]{1,0:T(8,128)S(1)}, f32[1024,768]{1,0:T(8,128)}, u32[]{:S(2)}) copy-start(f32[1024,768]{1,0:T(8,128)} %copy-done) | copy-start | bytes 9437188
  186.7 9.8 %copy-start.7 = (f32[1024,768]{1,0:T(8,128)S(1)}, f32[1024,768]{1,0:T(8,128)}, u32[]{:S(2)}) copy-start(f32[1024,768]{1,0:T(8,128)} %get-tuple-element.58) | copy-start | bytes 9437188
  186.7 9.8 %copy-start.15 = (bf16[1024,3072]{1,0:T(8,128)(2,1)S(1)}, bf16[1024,3072]{1,0:T(8,128)(2,1)}, u32[]{:S(2)}) copy-start(bf16[1024,3072]{1,0:T(8,128)(2,1)} %get-tuple-element.76) | copy-start | bytes 18874372
  206.7 3.7 copy-start.16
  210.4 7.8 %copy-start.8 = (f32[1024,768]{1,0:T(8,128)}, f32[1024,768]{1,0:T(8,128)S(1)}, u32[]{:S(2)}) copy-start(f32[1024,768]{1,0:T(8,128)S(1)} %get-tuple-element.60) | copy-start | bytes 9437188
  210.4 7.8 %copy-start.13 = (bf16[1024,768]{1,0:T(8,128)(2,1)S(1)}, bf16[1024,768]{1,0:T(8,128)(2,1)}, u32[]{:S(2)}) copy-start(bf16[1024,768]{1,0:T(8,128)(2,1)} %get-tuple-element.29) | copy-start | bytes 4718596
  218.2 2.7 copy-start.14
  244.2 4.6 %copy-start.9 = (f32[1024,768]{1,0:T(8,128)S(1)}, f32[1024,768]{1,0:T(8,128)}, u32[]{:S(2)}) copy-start(f32[1024,768]{1,0:T(8,128)} %copy-done.8) | copy-start | bytes 9437188
  244.2 5.5 %copy-start.11 = (bf16[4,2,2,3,16,2304]{5,4,3,2,1,0:T(8,128)(2,1)S(1)}, bf16[4,2,2,3,16,2304]{5,4,3,2,1,0:T(8,128)(2,1)}, u32[]{:S(2)}) copy-start(bf16[4,2,2,3,16,2304]{5,4,3,2,1,0:T(8,128)(2,1)} %get-tuple-element.27) | copy-start | bytes 10616836
  247.0 1.2 copy-start.3
  247.0 1.7 copy-start.5
  266.0 2.4 copy-start.4
  266.0 2.8 copy-start.6
  266.0 3.3 copy-start.12
  381.5 9.5 %copy-start.10 = (f32[2,3,64,768]{3,2,1,0:T(8,128)S(1)}, f32[2,3,64,768]{3,2,1,0:T(8,128)}, u32[]{:S(2)}) copy-start(f32[2,3,64,768]{3,2,1,0:T(8,128)} %get-tuple-element.39) | copy-start | bytes 3538948

commit v3 on v2

--- a/solution.py
+++ b/solution.py
@@ -522,6 +522,136 @@
     )(projected, projected, projected, grad_mixed, long_probs, short_probs)
 
 
+def gelu_pair(value):
+    size = jnp.abs(value)
+    bell = jnp.exp(-0.5 * value * value)
+    t = 1.0 / (1.0 + 0.23164189 * size)
+    tail = t * (0.127414796 + t * (-0.142248368 + t * (0.7107068705 + t * (-0.7265760135 + t * 0.5307027145))))
+    tail = tail * bell
+    whole = jnp.where(value >= 0.0, 1.0 - tail, tail)
+    return (value * whole, whole + value * bell * 0.3989422804)
+
+
+def middle_kernel(
+    step, span, mixed, tokens, cot, w_out, w_up, w_down, gains, biases, ff_bias,
+    out, acc, g_mixed, d_out, d_up, d_down, sums, d_ffb, unit, low, low2, hidden, slope, inv
+):
+    rows = mixed.shape[0]
+    parts = w_up.shape[1] // span
+    sums[...] = jnp.zeros_like(sums)
+
+    def rows_at(i):
+        return pl.ds(pl.multiple_of(i * step, step), step)
+
+    def columns_at(j):
+        return pl.ds(pl.multiple_of(j * span, span), span)
+
+    def mean(a):
+        return jnp.mean(a, axis=-1, keepdims=True)
+
+    def tally(i, a):
+        sums[i : i + 1, :] += jnp.sum(a, axis=0, keepdims=True)
+
+    def norm(r):
+        center = r - mean(r)
+        scale = lax.rsqrt(mean(center * center) + norm_eps)
+        return center * scale, scale
+
+    def back(s, u, scale):
+        return scale * (s - mean(s) - u * mean(s * u))
+
+    @pl.loop(0, rows // step)
+    def _(i):
+        at = rows_at(i)
+        branch = dot(mixed[at, :], w_out[...]) + biases[2:3, :]
+        u, scale = norm(tokens[at, :].astype(F32) + branch)
+        unit[at, :] = u
+        inv[at, :] = scale
+        low[at, :] = (u * gains[0:1, :] + biases[4:5, :]).astype(BF)
+        acc[at, :] = jnp.zeros((step, acc.shape[1]), F32)
+
+    @pl.loop(0, parts)
+    def _(j):
+        cols = columns_at(j)
+        for i in range(rows // step):
+            at = slice(i * step, (i + 1) * step)
+            inner = dot(low[at, :], w_up[:, cols]) + ff_bias[:, cols]
+            act, der = gelu_pair(inner)
+            act = act.astype(BF)
+            hidden[at, cols] = act
+            slope[at, cols] = der.astype(BF)
+            acc[at, :] += dot(act, w_down[cols, :])
+
+    @pl.loop(0, rows // step)
+    def _(i):
+        at = rows_at(i)
+        first = unit[at, :] * gains[0:1, :] + biases[4:5, :]
+        u, scale = norm(first + acc[at, :] + biases[3:4, :])
+        out[at, :] = (u * gains[1:2, :] + biases[5:6, :]).astype(BF)
+        g = cot[at, :].astype(F32)
+        tally(1, g * u)
+        tally(5, g)
+        g = back(g * gains[1:2, :], u, scale)
+        acc[at, :] = g
+        g = g.astype(BF)
+        low2[at, :] = g
+        tally(3, g.astype(F32))
+
+    @pl.loop(0, parts)
+    def _(j):
+        cols = columns_at(j)
+        total = None
+        for i in range(rows // step):
+            at = slice(i * step, (i + 1) * step)
+            g = dot(low2[at, :], w_down[cols, :], NT) * slope[at, cols].astype(F32)
+            g = g.astype(BF)
+            slope[at, cols] = g
+            part = jnp.sum(g.astype(F32), axis=0, keepdims=True)
+            total = part if total is None else total + part
+            acc[at, :] += dot(g, w_up[:, cols], NT)
+        d_ffb[:, cols] = total
+        d_down[cols, :] = dot(hidden[:, cols], low2[...], TN).astype(BF)
+        d_up[:, cols] = dot(low[...], slope[:, cols], TN).astype(BF)
+
+    @pl.loop(0, rows // step)
+    def _(i):
+        at = rows_at(i)
+        g, u = acc[at, :], unit[at, :]
+        tally(0, g * u)
+        tally(4, g)
+        g = back(g * gains[0:1, :], u, inv[at, :])
+        acc[at, :] = g
+        g = g.astype(BF)
+        low2[at, :] = g
+        tally(2, g.astype(F32))
+        g_mixed[at, :] = dot(g, w_out[...], NT).astype(BF)
+
+    d_out[...] = dot(mixed[...], low2[...], TN).astype(BF)
+
+
+def middle(mixed, tokens, cot, w_out, w_up, w_down, gains, biases, ff_bias):
+    rows, width = mixed.shape
+    ff = w_up.shape[1]
+    shape = jax.ShapeDtypeStruct
+    return pl.pallas_call(
+        functools.partial(middle_kernel, 256, 512),
+        out_shape=(
+            shape((rows, width), BF), shape((rows, width), F32), shape((rows, width), BF),
+            shape((width, width), BF), shape((width, ff), BF), shape((ff, width), BF),
+            shape((8, width), F32), shape((1, ff), F32),
+        ),
+        in_specs=[vm()] * 9,
+        out_specs=(vm(),) * 8,
+        scratch_shapes=[
+            pltpu.VMEM((rows, width), F32), pltpu.VMEM((rows, width), BF),
+            pltpu.VMEM((rows, width), BF), pltpu.VMEM((rows, ff), BF),
+            pltpu.VMEM((rows, ff), BF), pltpu.VMEM((rows, 1), F32),
+        ],
+        compiler_params=params(),
+        name="middle",
+    )(mixed, tokens, cot, w_out, w_up, w_down, gains, biases, ff_bias)
+
+
 def square():
     return lax.axis_size("dp") == 8 and lax.axis_size("rep") == 4
 
@@ -585,22 +715,6 @@
         own[:n0].reshape(d_gains.shape[0], -1),
         own[n0 : n0 + n1].reshape(d_biases.shape[0], -1),
         own[n0 + n1 : n0 + n1 + n2],
-    )
-
-
-def normalize_keep(residual, gain_row, shift_row):
-    center = residual - jnp.mean(residual, axis=-1, keepdims=True)
-    scale_inv = lax.rsqrt(jnp.mean(center * center, axis=-1, keepdims=True) + norm_eps)
-    unit_rows = center * scale_inv
-    return (unit_rows * gain_row + shift_row, unit_rows, scale_inv)
-
-
-def normalize_back(grad_in, unit_rows, scale_inv, gain_row):
-    scaled = grad_in * gain_row
-    return scale_inv * (
-        scaled
-        - jnp.mean(scaled, axis=-1, keepdims=True)
-        - unit_rows * jnp.mean(scaled * unit_rows, axis=-1, keepdims=True)
     )
 
 
@@ -635,43 +749,11 @@
         jnp.bfloat16
     )
     mixed_rows, long_probs, short_probs = attend(tab, projected)
-    branch = jnp.dot(mixed_rows, w_out, preferred_element_type=jnp.float32) + shift_rows[2]
-    first_norm, unit_one, inv_one = normalize_keep(
-        tokens.astype(jnp.float32) + branch, gain_rows[0], shift_rows[4]
-    )
-    first_low = first_norm.astype(jnp.bfloat16)
-    inner_pre = jnp.dot(first_low, w_up, preferred_element_type=jnp.float32) + up_bias
-    activated, gelu_pull = jax.vjp(lambda values: jax.nn.gelu(values, approximate=False), inner_pre)
-    hidden = activated.astype(jnp.bfloat16)
-    ffn_out = jnp.dot(hidden, w_down, preferred_element_type=jnp.float32) + shift_rows[3]
-    final_norm, unit_two, inv_two = normalize_keep(
-        first_norm + ffn_out, gain_rows[1], shift_rows[5]
-    )
-    output = unperm(tab, final_norm.astype(BF), per)
-    grad_out = cotangent.astype(jnp.float32)
-    d_gain_two = jnp.sum(grad_out * unit_two, axis=0)
-    d_shift_two = jnp.sum(grad_out, axis=0)
-    grad_two = normalize_back(grad_out, unit_two, inv_two, gain_rows[1])
-    grad_ffn = grad_two.astype(jnp.bfloat16)
-    d_down_bias = jnp.sum(grad_ffn.astype(jnp.float32), axis=0)
-    d_down = jnp.einsum("tf,td->fd", hidden, grad_ffn, preferred_element_type=jnp.float32)
-    grad_hidden = jnp.einsum("td,fd->tf", grad_ffn, w_down, preferred_element_type=jnp.float32)
-    grad_inner = gelu_pull(grad_hidden)[0].astype(jnp.bfloat16)
-    d_up_bias = jnp.sum(grad_inner.astype(jnp.float32), axis=0)
-    d_up = jnp.einsum("td,tf->df", first_low, grad_inner, preferred_element_type=jnp.float32)
-    grad_first = grad_two + jnp.einsum(
-        "tf,df->td", grad_inner, w_up, preferred_element_type=jnp.float32
-    )
-    d_gain_one = jnp.sum(grad_first * unit_one, axis=0)
-    d_shift_one = jnp.sum(grad_first, axis=0)
-    grad_one = normalize_back(grad_first, unit_one, inv_one, gain_rows[0])
-    grad_branch = grad_one.astype(jnp.bfloat16)
-    d_out_bias = jnp.sum(grad_branch.astype(jnp.float32), axis=0)
-    d_out = jnp.einsum("td,te->de", mixed_rows, grad_branch, preferred_element_type=jnp.float32)
-    grad_mixed = jnp.einsum(
-        "te,de->td", grad_branch, w_out, preferred_element_type=jnp.float32
-    ).astype(jnp.bfloat16)
-
+    final, grad_one, grad_mixed, d_out, d_up, d_down, sums, d_up_bias = middle(
+        mixed_rows, tokens, cotangent, w_out, w_up, w_down, gain_rows, shift_rows, up_bias[None]
+    )
+    d_up_bias = d_up_bias[0]
+    output = unperm(tab, final, per)
     parts = attend_back(projected, grad_mixed, long_probs, short_probs)
     grad_heads = jnp.concatenate([parts[0], parts[1], parts[2]], 1)
     d_head_bias = jnp.sum(grad_heads.astype(jnp.float32), axis=0)
@@ -680,16 +762,9 @@
         "te,de->td", grad_heads, w_qkv, preferred_element_type=jnp.float32
     )
     grad_tokens = unperm(tab, grad_tokens, per)
-    d_gains = jnp.stack([d_gain_one, d_gain_two])
-    d_biases = jnp.stack(
-        [
-            d_head_bias[:model_width],
-            d_head_bias[2 * model_width :],
-            d_out_bias,
-            d_down_bias,
-            d_shift_one,
-            d_shift_two,
-        ]
+    d_gains = sums[0:2]
+    d_biases = jnp.concatenate(
+        [d_head_bias[None, :model_width], d_head_bias[None, 2 * model_width :], sums[2:6]]
     )
     return (output, grad_tokens) + reduce_layer(d_qkv, d_out, d_up, d_down, d_gains, d_biases, d_up_bias)
 

time: 399 us -> 350 us (0.88); the launches traced: 393 us -> 349 us
  matrix products: 118 us -> 25.8 us
  Pallas kernels: 236 us -> 299 us
  other arithmetic: 12.1 us -> 1.86 us
    dot_general x9 -> x0, matrix products: 98 us -> none  [the longest x1 35.3 us: local(): jnp.dot(first_low, w_up, preferred_element_type=jnp.float32) + up_bias]
    pallas_call x0 -> x1, Pallas kernels: none -> 63.5 us  [middle(): pl.pallas_call(functools.partial(middle_kernel, 256, 512), out_shape=(sha...]
    reduce_sum x5 -> x0, other arithmetic: 9.54 us -> none  [the longest x1 4 us: local(): d_down_bias = jnp.sum(grad_ffn.astype(jnp.float32), axis=0)]
    unnamed x50 -> x19, local copies, waits for them, and re-layouts: 13.3 us -> 8.73 us
where the time goes in v3:
time: 350 us; the launch traced here: 349 us
  Pallas kernels  299 us (85%)
  matrix products  25.8 us (7%)
  local copies, waits for them, and re-layouts  21.3 us (6%)
    pallas_call x1, Pallas kernels, scatter(): pl.pallas_call(functools.partial(scatter_kernel, n), out_shape=[jax.Shape...  105 us
    pallas_call x1, Pallas kernels, gather(): pl.pallas_call(functools.partial(gather_kernel, n), out_shape=[jax.ShapeD...  76.9 us
    pallas_call x1, Pallas kernels, middle(): pl.pallas_call(functools.partial(middle_kernel, 256, 512), out_shape=(sha...  63.5 us
    pallas_call x1, Pallas kernels, attend_back(): pl.pallas_call(functools.partial(attend_back_kernel, HD ** (-0.5)), grid=...  18.7 us
    pallas_call x1, Pallas kernels, attend(): pl.pallas_call(functools.partial(attend_kernel, HD ** (-0.5)), grid=(pair...  15.3 us
    pallas_call x2, Pallas kernels, unperm(): pl.pallas_call(functools.partial(unperm_kernel, per), out_shape=jax.Shape...  10.6 us
    dot_general x1, matrix products, local(): jnp.einsum('te,de->td', grad_heads, w_qkv, preferred_element_type=jnp.flo...  9.36 us
    pallas_call x1, Pallas kernels, prep(): pl.pallas_call(functools.partial(prep_kernel, per), out_shape=(jax.ShapeD...  9.08 us

profile of v3, /device:TPU:0, one launch (start us, length us, event | category | flops | bytes accessed | tf_op | source)
XLA Modules:
  0.0 349.2 jit_solution(7681209548609639903)
XLA Ops:
  0.6 0.8 reshape.138
  1.4 0.7 reshape.139
  2.1 0.8 concatenate.22
  2.9 0.6 pad.8
  3.5 76.9 %gather.1 = (bf16[4,2,2,3,16,128]{5,4,3,2,1,0:T(8,128)(2,1)}, bf16[4,2,2,3,16,2304]{5,4,3,2,1,0:T(8,128)(2,1)}, bf16[4,2,2,3,16,768]{5,4,3,2,1,0:T(8,128)(2,1)},...) custom-call(bf16[2,3,16,128]{3,2,1,0:T(8,128)(2,1)} %bitcast.66, ...), custom_call_target="tpu_custom_call" | custom-call | tf_op jit(solution)/shard_map/gather/pallas_call | solution.py:272
  80.5 1.0 reshape_reshape.13
  81.5 0.1 reshape.161
  81.6 0.1 squeeze.15
  81.7 0.1 squeeze.16
  81.8 9.1 %prep.1 = (bf16[1024,768]{1,0:T(8,128)(2,1)}, bf16[1024,768]{1,0:T(8,128)(2,1)}, s32[1,128]{1,0:T(1,128)}) custom-call(s32[1]{0:T(128)} %bitcast.me_ref, s32[288]{0:T(512)} %own_ref.1, s32[288]{0:T(512)} %len_ref.1, bf16[1024,768]{1,0:T(8,128)(2,1)} %tok_ref.1, bf16[1024,768]{1,0:T(8,128)(2,1)} %cot_ref.1), custom_call_target="tpu_custom_call" | custom-call | tf_op jit(solution)/shard_map/prep/pallas_call | solution.py:104
  90.9 8.5 %add_convert_fusion.q_ref.k_ref.v_ref = bf16[1024,2304]{1,0:T(8,128)(2,1)} fusion(bf16[1024,768]{1,0:T(8,128)(2,1)} %get-tuple-element.34.tokens, bf16[768,2304]{1,0:T(8,128)(2,1)} %bitcast.71, f32[2304]{0:T(1024)S(1)} %pad_maximum_fusion.1), kind=kOutput, calls=%fused_computation.1 | convolution fusion | flops 3628597248 | bytes 9839616 | tf_op jit(solution)/shard_map/dot_general | solution.py:748
  99.3 15.3 %attend.1 = (bf16[1024,768]{1,0:T(8,128)(2,1)}, bf16[12,512,512]{2,1,0:T(8,128)(2,1)}, bf16[12,512,128]{2,1,0:T(8,128)(2,1)}) custom-call(s32[1,128]{1,0:T(1,128)} %get-tuple-element.33.tab_ref, bf16[1024,2304]{1,0:T(8,128)(2,1)} %add_convert_fusion.q_ref.k_ref.v_ref, bf16[1024,2304]{1,0:T(8,128)(2,1)} %add_convert_fusion.q_ref.k_ref.v_ref, ...), custom_call_target="tpu_custom_call" | custom-call | tf_op jit(solution)/shard_map/attend/pallas_call | solution.py:461
  114.6 0.7 convert_element_type.52.biases
  115.3 0.1 slice_convert_fusion.1
  115.4 0.1 reshape.162
  115.5 0.7 reshape.159.gains
  116.2 0.6 copy.28
  116.8 63.5 %middle.1 = (bf16[1024,768]{1,0:T(8,128)(2,1)}, f32[1024,768]{1,0:T(8,128)}, bf16[1024,768]{1,0:T(8,128)(2,1)}, bf16[768,768]{1,0:T(8,128)(2,1)}, bf16[768,3072]...) custom-call(bf16[1024,768]{1,0:T(8,128)(2,1)} %get-tuple-element.37.mixed, ...), custom_call_target="tpu_custom_call" | custom-call | tf_op jit(solution)/shard_map/middle/pallas_call | solution.py:636
  180.2 18.7 %attend_back.1 = bf16[3,1024,768]{2,1,0:T(8,128)(2,1)} custom-call(bf16[1024,2304]{1,0:T(8,128)(2,1)} %add_convert_fusion.q_ref.k_ref.v_ref, bf16[1024,2304]{1,0:T(8,128)(2,1)} %add_convert_fusion.q_ref.k_ref.v_ref, bf16[1024,2304]{1,0:T(8,128)(2,1)} %add_convert_fusion.q_ref.k_ref.v_ref, bf16[1024,768]{1,0:T(8,128)(2,1)} %get-tuple-element.44.g_ref, ...), custom_call_target="tpu_custom_call" | custom-call | tf_op jit(solution)/shard_map/attend_back/pallas_call | solution.py:510
  199.0 2.7 slice_bitcast_fusion.2
  201.6 0.0 copy-start
  201.7 0.0 copy-start.1
  201.7 0.0 copy-start.4
  201.7 0.0 copy-start.5
  201.7 1.1 copy-done
  202.8 1.1 convert_reduce_fusion
  203.9 0.0 copy-done.1
  203.9 0.1 concatenate.25
  204.0 0.1 concatenate.26
  204.1 0.0 copy-done.4
  204.1 0.1 concatenate.27
  204.2 0.1 reshape.154
  204.3 0.1 reshape.152
  204.4 0.1 reshape.153
  204.5 0.5 broadcast.14
  205.0 0.0 copy-done.5
  205.0 0.7 reduce.11
  205.7 0.1 concatenate.29
  205.8 0.7 copy.29
  206.5 8.0 %convolution_convert_fusion = bf16[768,2304]{1,0:T(8,128)(2,1)} fusion(bf16[1024,768]{1,0:T(8,128)(2,1)} %get-tuple-element.34.tokens, bf16[1024,768]{1,0:T(8,128)(2,1)} %copy-done, bf16[1024,768]{1,0:T(8,128)(2,1)} %copy-done.1, bf16[1024,768]{1,0:T(8,128)(2,1)S(1)} %get-tuple-element.59), kind=kOutput, calls=%fused_computation.2 | convolution fusion | flops 3639803904 | bytes 9830400 | tf_op jit(solution)/shard_map/td,te->de/dot_general | solution.py:760
  214.5 105.2 %scatter.1 = (f32[2,3,64,768]{3,2,1,0:T(8,128)}, f32[2,3,16,3072]{3,2,1,0:T(8,128)}, f32[2,3,16,768]{3,2,1,0:T(8,128)}, f32[2,3,16,2304]{3,2,1,0:T(8,128)}, f32[2,3,8,128]{3,2,1,0:T(8,128)}) custom-call(bf16[4,2,2,3,64,768]{5,4,3,2,1,0:T(8,128)(2,1)} %bitcast.51, bf16[4,2,2,3,16,3072]{5,4,3,2,1,0:T(8,128)(2,1)} %bitcast.50, ...), custom_call_target="tpu_custom_call" | custom-call | tf_op jit(solution)/shard_map/scatter/pallas_call | solution.py:397
  319.7 0.8 slice.79
  320.5 0.6 slice.94
  321.1 0.6 slice.93
  321.7 1.3 slice.95
  323.0 9.4 %convolution_add_fusion.src_ref = f32[1024,768]{1,0:T(8,128)} fusion(f32[1024,768]{1,0:T(8,128)} %get-tuple-element.43, bf16[768,2304]{1,0:T(8,128)(2,1)} %bitcast.72, bf16[1024,768]{1,0:T(8,128)(2,1)} %copy-done, bf16[1024,768]{1,0:T(8,128)(2,1)} %copy-done.1, bf16[1024,768]{1,0:T(8,128)(2,1)S(1)} %get-tuple-element.59), kind=kOutput, calls=%fused_computation.4 | convolution fusion | flops 3638820864 | bytes 14548992 | tf_op jit(solution)/shard_map/te,de->td/dot_general | solution.py:761
  332.3 6.1 %unperm.3 = f32[1024,768]{1,0:T(8,128)} custom-call(s32[1,128]{1,0:T(1,128)} %get-tuple-element.33.tab_ref, f32[1024,768]{1,0:T(8,128)} %convolution_add_fusion.src_ref), custom_call_target="tpu_custom_call" | custom-call | tf_op jit(solution)/shard_map/unperm/pallas_call | solution.py:153
  338.4 0.0 copy-start.3
  338.4 0.0 copy-start.2
  338.5 4.5 %unperm.2 = bf16[1024,768]{1,0:T(8,128)(2,1)} custom-call(s32[1,128]{1,0:T(1,128)} %get-tuple-element.33.tab_ref, bf16[1024,768]{1,0:T(8,128)(2,1)} %get-tuple-element.42.src_ref), custom_call_target="tpu_custom_call" | custom-call | tf_op jit(solution)/shard_map/unperm/pallas_call | solution.py:153
  343.0 2.1 copy.36
  345.1 0.0 copy-done.3
  345.1 0.7 copy.37
  345.8 2.4 copy.38
  348.2 0.0 copy-done.2
  348.2 1.0 copy.39
  (15 shorter events, 0.1 us)
Async XLA Ops:
  201.6 1.2 copy-start
  201.7 2.3 copy-start.1
  201.7 2.4 copy-start.4
  201.7 3.3 copy-start.5
  338.4 6.7 %copy-start.3 = (f32[2,3,16,768]{3,2,1,0:T(8,128)S(1)}, f32[2,3,16,768]{3,2,1,0:T(8,128)}, u32[]{:S(2)}) copy-start(f32[2,3,16,768]{3,2,1,0:T(8,128)} %get-tuple-element.53) | copy-start | bytes 884740
  338.4 9.7 %copy-start.2 = (f32[2,3,64,768]{3,2,1,0:T(8,128)S(1)}, f32[2,3,64,768]{3,2,1,0:T(8,128)}, u32[]{:S(2)}) copy-start(f32[2,3,64,768]{3,2,1,0:T(8,128)} %get-tuple-element.55) | copy-start | bytes 3538948
